TPU v7x, 32 devices: a whole 2x2x4 slice. The times are simulated.
32 devices in a mesh: region: 4 (over x, core), domain: 8 (over z, y).
Axes of the slice: x: 2, y: 2, z: 4, core: 2. Of those that a mesh axis runs over, the one named last changes fastest.
Arguments:
- midpoints: float32 [3, 16384], P(None, ('region', 'domain')), may hold values from 0 to 1, as said below
- line_vectors: float32 [3, 16384], P(None, ('region', 'domain')), may hold values from -0.09375 to 0.09375
- burgers: float32 [3, 16384], P(None, ('region', 'domain')), may hold values from -4 to 4
- destination: int32 [16384, 1], P(('region', 'domain')), may hold values from 0 to 7; in each aligned block of 512 rows (0 to 511, 512 to 1023, ...) at most 128 rows name the same one
- node_ids: int32 [2, 16384], P(None, ('region', 'domain')), may hold values from 0 to 2047
- cell_ids: int32 [16384], P(('region', 'domain')), may hold values from 0 to 127, as said below
- cell_centers: float32 [3, 512], replicated, may hold values from 0 to 1, as said below
Outputs:
- slot_traction: float32 [3, 32768], P(None, ('region', 'domain'))
- nodal_force: float32 [3, 8192], P(None, ('region', 'domain'))
Inputs may be any that keep to these rules, and one draw needn't show every extreme that they name: `destination`: among the rows of one device, no domain is named by more than 128 rows, a bound that some block reaches. `cell_ids`: region r is the slab of x from r / 4 to (r + 1) / 4 of the unit cube; its 128 cells are the boxes of a 2 x 4 x (16) grid in that slab, numbered with the last grid index fastest. `cell_centers`: each cell's center lies within its box, within a quarter of the box's width of the box's middle along each dimension. `midpoints`: each segment's midpoint lies within its cell's box.
All inputs are finite; a program needn't handle non-finite values.
Results may differ from a plain program's by a relative error of at most 0.0003.
Values sent between devices are 32-bit elements; how exact they have to be, the bound alone decides.
No kernel may reach another device: no remote copies, remote signals or barrier semaphores. Data moves between devices by JAX's collectives and lax.ppermute only.
A program may use at most 64 MiB of HBM per device.

v0:
```python
import jax
import jax.numpy as jnp
from jax import lax
from jax.sharding import PartitionSpec as P

CELLS_REG = 128


CORE2 = 0.01
EXACT = lax.Precision.HIGHEST


def product(left, right):
    return jnp.dot(left, right, precision=EXACT, preferred_element_type=jnp.float32)


def source_terms(m, l, b):
    count = m.shape[1]
    outer = (b[:, None, :] * l[None, :, :]).reshape(9, count)
    q = jnp.cross(b, l, axis=0)
    qm = (q[:, None, :] * m[None, :, :]).reshape(9, count)
    return (outer, jnp.concatenate([qm, q], axis=0))


def pair_block(m, outer, second, targets):
    r2 = (targets[0][None, :] - m[0][:, None]) ** 2
    r2 = r2 + (targets[1][None, :] - m[1][:, None]) ** 2
    r2 = r2 + (targets[2][None, :] - m[2][:, None]) ** 2
    g1 = 1.0 / jnp.sqrt(r2 + CORE2)
    g3 = g1 * g1 * g1
    first = product(outer, g1)
    other = product(second, g3)
    cross_part = (other[9:12][:, None, :] * targets[None, :, :]).reshape(9, targets.shape[1])
    return first + cross_part - other[0:9]


def moment_terms(m, l, b, centers):
    count = m.shape[1]
    outer = (b[:, None, :] * l[None, :, :]).reshape(9, count)
    offset = m - centers
    dipole = (outer[:, None, :] * offset[None, :, :]).reshape(27, count)
    q = jnp.cross(b, l, axis=0)
    return jnp.concatenate([outer, dipole, q], axis=0)


def far_field(moments, centers, region_centers, region, cells_reg):
    total = centers.shape[1]
    diffs = [region_centers[a][None, :] - centers[a][:, None] for a in range(3)]
    r2 = diffs[0] ** 2 + diffs[1] ** 2 + diffs[2] ** 2
    keep = (jnp.arange(total, dtype=jnp.int32) // cells_reg != region).astype(jnp.float32)
    g1 = keep[:, None] / jnp.sqrt(r2 + CORE2)
    g3 = g1 * g1 * g1
    field = product(moments[0:9], g1)
    pulls = []
    for axis_a in range(3):
        weighted = diffs[axis_a] * g3
        field = field + product(moments[9 + axis_a : 36 : 3], weighted)
        pulls.append(product(moments[36:39], weighted))
    nterm = jnp.stack(pulls, axis=1).reshape(9, region_centers.shape[1])
    return field + nterm


def traction(stress, b):
    count = stress.shape[1]
    sigma = stress.reshape(3, 3, count)
    sym = 0.5 * (sigma + jnp.transpose(sigma, (1, 0, 2)))
    return jnp.sum(sym * b[None, :, :], axis=1)


def fold_blocks(total_stress, rows, block_fn):
    width = rows.shape[1]
    if width <= 1024 or width % 512 != 0:
        return total_stress + block_fn(rows)
    split = jnp.transpose(rows.reshape(rows.shape[0], width // 512, 512), (1, 0, 2))

    def step(carry, part):
        return (carry + block_fn(part), None)

    result, _ = lax.scan(step, total_stress, split)
    return result


def body(midpoints, line_vectors, burgers, destination, node_ids, cell_ids, cell_centers):
    count = midpoints.shape[1]
    domains = lax.axis_size("domain")
    capacity = 2 * count // domains
    slots = 2 * count
    region = lax.axis_index("region")
    region_centers = lax.dynamic_slice_in_dim(cell_centers, region * CELLS_REG, CELLS_REG, 1)
    cell_table = (jnp.arange(CELLS_REG, dtype=jnp.int32)[:, None] == cell_ids[None, :]).astype(
        jnp.float32
    )
    seg_centers = product(region_centers, cell_table)
    feats = moment_terms(midpoints, line_vectors, burgers, seg_centers)
    partial_value = product(feats, cell_table.T)
    summed = lax.psum(partial_value, "domain")
    moments = lax.all_gather(summed, "region", axis=1, tiled=True)
    far = far_field(moments, cell_centers, region_centers, region, CELLS_REG)

    def near_stress(targets):
        empty = jnp.zeros((9, targets.shape[1]), jnp.float32)
        outer, second = source_terms(midpoints, line_vectors, burgers)
        payload = jnp.concatenate([midpoints, outer, second], axis=0)

        def expanded_block(rows):
            return pair_block(rows[0:3], rows[3:12], rows[12:24], targets)

        return fold_blocks(
            empty, lax.all_gather(payload, "domain", axis=1, tiled=True), expanded_block
        )

    dest = destination[:, 0]
    hot = (dest[:, None] == jnp.arange(domains, dtype=jnp.int32)[None, :]).astype(jnp.int32)
    rank = jnp.sum(jnp.cumsum(hot, axis=0) * hot, axis=1) - 1
    slot = dest * capacity + rank
    stress = near_stress(midpoints) + product(far, cell_table)
    force = traction(stress, burgers)
    outgoing = jnp.zeros((3, slots), jnp.float32).at[:, slot].set(force)
    slot_traction = lax.all_to_all(outgoing, "domain", split_axis=1, concat_axis=1, tiled=True)
    half = 0.5 * force
    node_partial = jnp.zeros((3, count // 2 * domains), jnp.float32)
    node_partial = node_partial.at[:, node_ids[0]].add(half).at[:, node_ids[1]].add(half)
    nodal_force = lax.psum_scatter(node_partial, "domain", scatter_dimension=1, tiled=True)
    return (slot_traction, nodal_force)


def solution(mesh):
    in_specs = (
        P(None, ("region", "domain")),
        P(None, ("region", "domain")),
        P(None, ("region", "domain")),
        P(("region", "domain"), None),
        P(None, ("region", "domain")),
        P(("region", "domain")),
        P(),
    )
    out_specs = (P(None, ("region", "domain")), P(None, ("region", "domain")))
    return jax.shard_map(body, mesh=mesh, in_specs=in_specs, out_specs=out_specs, check_vma=False)
```

profile of v0, /device:TPU:0, one launch (start us, length us, event | category | flops | bytes accessed | tf_op | source)
XLA Modules:
  0.0 186.8 jit_solution(9238915904574163798)
XLA Ops:
  9.8 38.9 %psum.7 = f32[39,128]{1,0:T(8,128)S(1)} all-reduce(f32[39,128]{1,0:T(8,128)S(1)} %fusion.27), channel_id=1, replica_groups=mesh['region'=4,'domain'=8] {'domain'}, use_global_device_ids=true, to_apply=%region_5.7 | all-reduce | flops 4992 | bytes 39936 | tf_op jit(solution)/shard_map/psum | solution.py:96
  48.7 5.3 %all_gather.7 = f32[39,512]{1,0:T(8,128)S(1)} all-gather(f32[39,128]{1,0:T(8,128)S(1)} %psum.7), channel_id=1, replica_groups=mesh['region'=4,'domain'=8] {'region'}, dimensions={1}, use_global_device_ids=true | all-gather | bytes 99840 | tf_op jit(solution)/shard_map/all_gather | solution.py:97
  56.4 31.0 %all_gather.6 = f32[24,4096]{1,0:T(8,128)S(1)} all-gather(f32[24,512]{1,0:T(8,128)S(1)} %maximum_maximum_fusion), channel_id=1, replica_groups=mesh['region'=4,'domain'=8] {'domain'}, dimensions={1}, use_global_device_ids=true | all-gather | bytes 442368 | tf_op jit(solution)/shard_map/all_gather | solution.py:109
  87.6 18.2 %while.11 = (s32[]{:T(128)}, f32[9,512]{1,0:T(8,128)S(1)}, f32[8,24,512]{2,0,1:T(8,128)S(1)}, f32[3,512]{1,0:T(4,128)S(1)}, s32[]{:T(128)}, /*index=5*/s32[]{:T(128)}, s32[]{}, s32[]{}, s32[]{}, s32[]{}) while((s32[]{:T(128)}, f32[9,512]{1,0:T(8,128)S(1)}, f32[8,24,512]{2,0,1:T(8,128)S(1)}, f32[3,512]{1,0:T(4,128)S(1)}, s32[]{:T(128)}, ...), condition=%wide.region_4.6_spmd.clone, body=%wide.region_3.5_spmd.clone.sunk | while | flops 71326208 | bytes 356539 | solution.py:79
  87.6 1.1 fusion.96
  88.8 1.0 fusion.97
  89.9 1.1 fusion.96
  92.2 1.1 fusion.96
  93.4 1.0 fusion.97
  94.5 1.1 fusion.96
  95.6 1.0 fusion.97
  96.7 1.1 fusion.96
  97.9 1.0 fusion.97
  99.0 1.1 fusion.96
  101.3 1.1 fusion.96
  103.6 1.1 fusion.96
  104.7 1.0 fusion.97
  108.4 2.5 %scatter_custom_fusion.1 = f32[3,2048]{0,1:T(8,128)S(1)} fusion(s32[512]{0:T(512)S(1)} %bitcast.138, f32[512,3]{1,0:T(8,128)S(1)} %copy.28, f32[]{:T(128)} %constant.24.clone.1), kind=kCustom, calls=%fused_computation.42 | custom fusion | flops 1536 | bytes 24580 | tf_op jit(solution)/shard_map/scatter-add | solution.py:122
  110.9 3.7 %scatter_fusion = f32[3,2048]{0,1:T(8,128)S(1)} fusion(f32[3,2048]{0,1:T(8,128)S(1)} %scatter_custom_fusion.1, s32[512]{0:T(512)S(1)} %bitcast.114, f32[512,3]{1,0:T(8,128)S(1)} %copy.28), kind=kCustom, calls=%fused_computation.2 | custom fusion | flops 1536 | bytes 20480 | tf_op jit(solution)/shard_map/scatter-add | solution.py:122
  115.6 1.1 reduce-window.6
  117.3 1.8 scatter_custom_fusion
  119.3 9.0 %all_to_all.12 = f32[3,8,128]{2,0,1:T(4,128)S(1)} all-to-all(f32[3,8,128]{2,0,1:T(4,128)S(1)} %copy.27), channel_id=1, replica_groups=mesh['region'=4,'domain'=8] {'domain'}, dimensions={1} | all-to-all | bytes 24576 | tf_op jit(solution)/shard_map/all_to_all | solution.py:119
  128.4 49.4 %reduce-scatter.2.cloned.1.call-done = f32[3,256]{0,1:T(8,128)} async-done(((f32[3,2048]{0,1:T(8,128)}), f32[3,256]{0,1:T(8,128)}) %reduce-scatter.2.cloned.1.call-update) | async-done | bytes 3088 | tf_op jit(solution)/shard_map/reduce_scatter | solution.py:123
  177.7 1.6 copy.30
  (124 shorter events, 13.9 us)
Async XLA Ops:
  7.2 0.7 copy-start.5
  7.2 170.6 %reduce-scatter.2.cloned.1.call-start = ((), (), s32[]{:S(2)}) async-start(), calls=%async_computation.2 | async-start | bytes 1179648 | tf_op jit(solution)/shard_map/reduce_scatter | solution.py:123
  7.9 0.7 copy-start.2
  7.9 0.7 copy-start.3
  8.6 0.7 copy-start.1
  8.6 0.7 copy-start.7
  107.7 0.7 copy-start.6
  114.6 1.0 copy-start
  114.6 1.0 copy-start.4
Sparse Core Ops, SparseCore 0:
  115.7 61.9 reduce-scatter.1
where the time goes:
time: 187 us
  blocking collectives  84.1 us (45%)
  waiting for transfers between devices  49.4 us (26%)
  matrix products  21.4 us (11%)
  between operations  14.3 us (8%)
  local copies, waits for them, and re-layouts  9.35 us (5%)
  other arithmetic  7.69 us (4%)
    reduce_scatter x1, waiting for transfers between devices, body(): lax.psum_scatter(node_partial, 'domain', scatter_dimension=1, tiled=True)  49.4 us
    psum x1, blocking collectives, body(): summed = lax.psum(partial_value, 'domain')  38.9 us
    all_gather x1, blocking collectives, near_stress(): lax.all_gather(payload, 'domain', axis=1, tiled=True)  31 us
    dot_general x26, matrix products, product(): jnp.dot(left, right, precision=EXACT, preferred_element_type=jnp.float32)  21.4 us
    all_to_all x1, blocking collectives, body(): lax.all_to_all(outgoing, 'domain', split_axis=1, concat_axis=1, tiled=True)  9.02 us
    scatter-add x2, other arithmetic, body(): node_partial.at[:, node_ids[0]].add(half).at[:, node_ids[1]].add(half)  6.19 us
    unnamed x19, local copies, waits for them, and re-layouts  5.89 us
    all_gather x1, blocking collectives, body(): moments = lax.all_gather(summed, 'region', axis=1, tiled=True)  5.27 us
  transfers between devices with their start and end apart: 1, of which 1 were waited for; matrix products, arithmetic and copies ran while one was open for 2% of the time, Pallas kernels for 0%

commit v1 on v0

v1 whole, which is shorter than its diff:
```python
import functools

import jax
import jax.numpy as jnp
from jax import lax
from jax.experimental import pallas as pl
from jax.experimental.pallas import tpu as pltpu
from jax.sharding import PartitionSpec as P

CORE2 = 0.01
LANES = 128
F32 = jnp.float32
BF16 = jnp.bfloat16
SYM = ((0, 0), (1, 1), (2, 2), (0, 1), (0, 2), (1, 2))
SENT = 10
DIST_ROWS, FIRST_ROWS, SECOND_ROWS = 32, 16, 32
NEAR_ROWS = DIST_ROWS + FIRST_ROWS + SECOND_ROWS
MOMENT_ROWS = 32
VMEM_LIMIT = 32 << 20
VMEM_SPEC = pl.BlockSpec(memory_space=pltpu.VMEM)


def rounded(x):
    return x.astype(BF16).astype(F32)


def split2(x):
    high = rounded(x)
    return high, x - high


def split3(x):
    high = rounded(x)
    rest = x - high
    middle = rounded(rest)
    return high, middle, rest - middle


def dot(left, right):
    return jnp.dot(left, right, preferred_element_type=F32)


def dot_nt(left, right):
    return lax.dot_general(left, right, (((1,), (1,)), ((), ())), preferred_element_type=F32)


def middle_of(regions):
    region = lax.axis_index("region")
    return ((region.astype(F32) + 0.5) / regions, 0.5, 0.5)


def call(body, out_shape, inputs, flops, name):
    return pl.pallas_call(
        body,
        out_shape=out_shape,
        in_specs=[VMEM_SPEC] * len(inputs),
        out_specs=jax.tree.map(lambda _: VMEM_SPEC, out_shape),
        cost_estimate=pl.CostEstimate(flops=flops, bytes_accessed=1 << 16, transcendentals=0),
        compiler_params=pltpu.CompilerParams(vmem_limit_bytes=VMEM_LIMIT),
        name=name,
    )(*inputs)


def pack_body(m_ref, l_ref, b_ref, cell_ref, out_ref):
    quarters = m_ref.shape[1] // LANES
    parts = [ref[...] for ref in (m_ref, l_ref, b_ref)] + [cell_ref[...].astype(F32)]
    rows = [
        part[a : a + 1, q * LANES : (q + 1) * LANES]
        for part in parts
        for a in range(part.shape[0])
        for q in range(quarters)
    ]
    block = jnp.concatenate(rows, axis=0)
    for d in range(out_ref.shape[0]):
        out_ref[d] = block


def local_body(regions, domains, m_ref, dest_ref, nodes_ref, cell_ref, centers_ref, target_ref, hot_ref, cell_hot_ref, far_ref):
    count = m_ref.shape[1]
    cells = centers_ref.shape[1] // regions
    region = lax.axis_index("region")
    middle = middle_of(regions)
    x = [m_ref[a : a + 1, :] - middle[a] for a in range(3)]
    parts = [split3(-2.0 * v) for v in x]
    norm = split3(x[0] * x[0] + x[1] * x[1] + x[2] * x[2] + CORE2)
    ones = jnp.ones((1, count), F32)
    rows = [parts[a][p] for a in range(3) for p in (0, 1, 2, 0, 1, 0)]
    rows += [ones, ones, ones] + list(norm) + [jnp.zeros((DIST_ROWS - 24, count), F32)]
    target_ref[...] = jnp.concatenate(rows, axis=0).astype(BF16)
    dest = dest_ref[...]
    hot = (lax.broadcasted_iota(jnp.int32, (domains, count), 0) == dest).astype(BF16)
    earlier = (
        lax.broadcasted_iota(jnp.int32, (count, count), 0)
        < lax.broadcasted_iota(jnp.int32, (count, count), 1)
    ).astype(BF16)
    before = dot(hot, earlier)
    rank = jnp.sum(before * hot.astype(F32), axis=0, keepdims=True).astype(jnp.int32)
    slot = dest * LANES + rank
    ids = jnp.concatenate([slot, nodes_ref[...], jnp.zeros((5, count), jnp.int32)], axis=0).astype(F32)
    columns = jnp.transpose(ids).astype(jnp.int32)
    slots = domains * LANES
    wide = 1024
    for start in range(0, hot_ref.shape[1], wide):
        lane = lax.broadcasted_iota(jnp.int32, (count, wide), 1) + (start % slots if start < slots else start - slots)
        if start < slots:
            value = (lane == columns[:, 0:1]).astype(F32)
        else:
            value = 0.5 * (lane == columns[:, 1:2]).astype(F32) + 0.5 * (lane == columns[:, 2:3]).astype(F32)
        hot_ref[:, start : start + wide] = value.astype(BF16)
    cell_hot_ref[...] = (lax.broadcasted_iota(jnp.int32, (cells, count), 0) == cell_ref[...]).astype(BF16)
    here = centers_ref[:, pl.ds(pl.multiple_of(region * cells, cells), cells)]
    for k in range(1, regions):
        other = lax.bitwise_xor(region, k)
        there = centers_ref[:, pl.ds(pl.multiple_of(other * cells, cells), cells)]
        column = jnp.transpose(jnp.concatenate([there, jnp.zeros((5, cells), F32)], axis=0))
        d = [here[a : a + 1, :] - column[:, a : a + 1] for a in range(3)]
        g1 = lax.rsqrt(d[0] * d[0] + d[1] * d[1] + d[2] * d[2] + CORE2)
        g3 = g1 * g1 * g1
        for j, factor in enumerate([g1] + [v * g3 for v in d]):
            high, low = split2(factor)
            row = ((k - 1) * 4 + j) * cells
            far_ref[row : row + cells, 0:cells] = high.astype(BF16)
            far_ref[row : row + cells, cells : 2 * cells] = low.astype(BF16)


def source_body(regions, got_ref, centers_ref, near_ref, moment_ref, terms_ref, cell_rows_ref):
    sent_rows = SENT * 4
    devices = got_ref.shape[0] // sent_rows
    cells = moment_ref.shape[1]
    middle = middle_of(regions)
    zero = jnp.zeros((8, LANES), F32)
    one = jnp.ones((8, LANES), F32)
    quarters = 4
    for group in range(devices // 8):
        for quarter in range(quarters):

            def value(c):
                return got_ref[pl.ds(group * 8 * sent_rows + c * quarters + quarter, 8, stride=sent_rows), :]

            first_block = (group * quarters + quarter) * 8
            m = [value(a) - middle[a] for a in range(3)]
            l = [value(3 + a) for a in range(3)]
            b = [value(6 + a) for a in range(3)]
            q = [b[1] * l[2] - b[2] * l[1], b[2] * l[0] - b[0] * l[2], b[0] * l[1] - b[1] * l[0]]
            outer = [b[i] * l[i] if i == j else 0.5 * (b[i] * l[j] + b[j] * l[i]) for i, j in SYM]
            second = q + [q[i] * m[i] if i == j else 0.5 * (q[i] * m[j] + q[j] * m[i]) for i, j in SYM]
            parts = [split3(v) for v in m]
            norm = split3(m[0] * m[0] + m[1] * m[1] + m[2] * m[2])
            rows = [parts[a][p] for a in range(3) for p in (0, 0, 0, 1, 1, 2)]
            rows += list(norm) + [one, one, one] + [zero] * (DIST_ROWS - 24)
            pair = [split2(v) for v in outer]
            for p in range(2):
                rows += [v[p] for v in pair] + [None] * (FIRST_ROWS // 2 - 6)
            pair = [split2(v) for v in second]
            for p in range(2):
                rows += [v[p] for v in pair] + [None] * (SECOND_ROWS // 2 - 9)
            for f, row in enumerate(rows):
                near_ref[pl.ds(first_block * NEAR_ROWS + f, 8, stride=NEAR_ROWS), :] = zero if row is None else row
            terms = outer + [q[0], q[1]]
            for a in range(3):
                terms += [v * m[a] for v in outer] + ([q[2], zero] if a == 0 else [zero, zero])
            terms = [split3(v) for v in terms]
            for p in range(3):
                for f, row in enumerate(terms):
                    at = first_block * 3 * MOMENT_ROWS + p * MOMENT_ROWS + f
                    terms_ref[pl.ds(at, 8, stride=3 * MOMENT_ROWS), :] = row[p]
            cell_rows_ref[first_block : first_block + 8, :] = value(9).astype(jnp.int32)

    def step(i, total):
        left = [terms_ref[pl.ds(pl.multiple_of((2 * i + h) * 3 * MOMENT_ROWS, 8), 3 * MOMENT_ROWS), :] for h in range(2)]
        left = jnp.concatenate(left, axis=1).astype(BF16)
        rows = [cell_rows_ref[pl.ds(2 * i + h, 1), :] for h in range(2)]
        hot = jnp.concatenate(rows, axis=1) == lax.broadcasted_iota(jnp.int32, (cells, 2 * LANES), 0)
        return total + dot_nt(left, hot.astype(BF16))

    blocks = devices * quarters
    total = lax.fori_loop(0, blocks // 2, step, jnp.zeros((3 * MOMENT_ROWS, cells), F32), unroll=4)
    total = total[0:32] + total[32:64] + total[64:96]
    region = lax.axis_index("region")
    here = centers_ref[:, pl.ds(pl.multiple_of(region * cells, cells), cells)]
    charge = total[0:6]
    n = [total[6:7], total[7:8], total[14:15]]
    none = jnp.zeros((1, cells), F32)
    fold = [
        [n[0], none, none, 0.5 * n[1], 0.5 * n[2], none],
        [none, n[1], none, 0.5 * n[0], none, 0.5 * n[2]],
        [none, none, n[2], none, 0.5 * n[0], 0.5 * n[1]],
    ]
    pad = jnp.zeros((2, cells), F32)
    moment_ref[0:8, :] = jnp.concatenate([charge, pad], axis=0)
    for a in range(3):
        about = total[8 + 8 * a : 14 + 8 * a] - (here[a : a + 1, :] - middle[a]) * charge
        about = about + jnp.concatenate(fold[a], axis=0)
        moment_ref[8 + 8 * a : 16 + 8 * a, :] = jnp.concatenate([about, pad], axis=0)


def near_body(near_ref, target_ref, first_ref, second_ref):
    blocks = near_ref.shape[0] // NEAR_ROWS
    count = target_ref.shape[1]
    first_ref[...] = jnp.zeros_like(first_ref)
    second_ref[...] = jnp.zeros_like(second_ref)

    def step(i, carry):
        part = [near_ref[pl.ds(pl.multiple_of((2 * i + h) * NEAR_ROWS, 8), NEAR_ROWS), :] for h in range(2)]
        factors = jnp.concatenate([jnp.transpose(p[0:DIST_ROWS]) for p in part], axis=0).astype(BF16)
        rows = jnp.concatenate([p[DIST_ROWS:] for p in part], axis=1).astype(BF16)
        for start in range(0, count, 256):
            at = slice(start, start + 256)
            g1 = lax.rsqrt(dot(factors, target_ref[:, at]))
            g3 = g1 * g1 * g1
            high = g1.astype(BF16)
            low = (g1 - high.astype(F32)).astype(BF16)
            first_ref[:, at] += dot(rows[0:FIRST_ROWS], high) + dot(rows[0:FIRST_ROWS], low)
            high = g3.astype(BF16)
            low = (g3 - high.astype(F32)).astype(BF16)
            second_ref[:, at] += dot(rows[FIRST_ROWS:], high) + dot(rows[FIRST_ROWS:], low)
        return carry

    lax.fori_loop(0, blocks // 2, step, 0, unroll=2)


def stacked3(x):
    return jnp.concatenate(split3(x), axis=0).astype(BF16)


def force_body(regions, m_ref, b_ref, first_ref, second_ref, far_ref, cell_hot_ref, hot_ref, *rest):
    moment_refs, out_ref = rest[:-1], rest[-1]
    cells = moment_refs[0].shape[1]
    domains = out_ref.shape[0]
    middle = middle_of(regions)
    left = [ref[8 * j : 8 * j + 8, :] for ref in moment_refs for j in range(4)]
    left = stacked3(jnp.concatenate(left, axis=1))
    field = dot(left, far_ref[...])
    field = field[:, 0:cells] + field[:, cells:]
    field = field[0:8] + field[8:16] + field[16:24]
    field = dot(stacked3(field), cell_hot_ref[...])
    field = field[0:8] + field[8:16] + field[16:24]
    first = first_ref[...]
    second = second_ref[...]
    second = second[0:16] + second[16:32]
    x = [m_ref[a : a + 1, :] - middle[a] for a in range(3)]
    q = [second[a : a + 1] for a in range(3)]
    cross = [q[i] * x[i] if i == j else 0.5 * (q[i] * x[j] + q[j] * x[i]) for i, j in SYM]
    sigma = first[0:6] + first[8:14] + (jnp.concatenate(cross, axis=0) - second[3:9]) + field[0:6]
    at = {}
    for row, (i, j) in enumerate(SYM):
        at[i, j] = at[j, i] = sigma[row : row + 1]
    b = [b_ref[a : a + 1, :] for a in range(3)]
    force = [at[i, 0] * b[0] + at[i, 1] * b[1] + at[i, 2] * b[2] for i in range(3)]
    force = jnp.concatenate(force + [jnp.zeros((5, b[0].shape[1]), F32)], axis=0)
    spread = dot(stacked3(force), hot_ref[...])
    spread = spread[0:3] + spread[8:11] + spread[16:19]
    slots = domains * LANES
    own = (spread.shape[1] - slots) // domains
    for d in range(domains):
        pieces = [spread[:, d * LANES : (d + 1) * LANES]]
        for h in range(own // LANES):
            pieces.append(spread[:, slots + d * own + h * LANES : slots + d * own + (h + 1) * LANES])
        used = 3 * len(pieces)
        pieces.append(jnp.zeros((out_ref.shape[1] - used, LANES), F32))
        out_ref[d] = jnp.concatenate(pieces, axis=0)


def collect_body(got_ref, slot_ref, node_ref):
    domains = got_ref.shape[0]
    capacity = slot_ref.shape[1] // domains
    total = jnp.sum(got_ref[...], axis=0)
    for d in range(domains):
        slot_ref[:, d * capacity : (d + 1) * capacity] = got_ref[d, 0:3, 0:capacity]
    for h in range(node_ref.shape[1] // LANES):
        node_ref[:, h * LANES : (h + 1) * LANES] = total[3 + 3 * h : 6 + 3 * h]


def body(midpoints, line_vectors, burgers, destination, node_ids, cell_ids, cell_centers):
    count = midpoints.shape[1]
    domains = lax.axis_size("domain")
    regions = lax.axis_size("region")
    cells = cell_centers.shape[1] // regions
    nodes = count // 2 * domains
    own = nodes // domains
    cell_row = cell_ids.reshape(1, count)
    dest_row = destination.reshape(1, count)
    shape = jax.ShapeDtypeStruct
    quarters = count // LANES
    payload = call(
        pack_body,
        shape((domains, SENT * quarters, LANES), F32),
        (midpoints, line_vectors, burgers, cell_row),
        1 << 12,
        "pack",
    )
    got = lax.all_to_all(payload, "domain", split_axis=0, concat_axis=0, tiled=True)
    far_rows = (regions - 1) * 4 * cells
    target, hot, cell_hot, far = call(
        functools.partial(local_body, regions, domains),
        (
            pltpu.VMEM((DIST_ROWS, count), BF16),
            pltpu.VMEM((count, domains * LANES + nodes), BF16),
            pltpu.VMEM((cells, count), BF16),
            pltpu.VMEM((far_rows, 2 * cells), BF16),
        ),
        (midpoints, dest_row, node_ids, cell_row, cell_centers),
        1 << 30,
        "local",
    )
    blocks = domains * quarters
    near, moments = pl.pallas_call(
        functools.partial(source_body, regions),
        out_shape=(pltpu.VMEM((blocks * NEAR_ROWS, LANES), F32), shape((MOMENT_ROWS, cells), F32)),
        in_specs=[VMEM_SPEC] * 2,
        out_specs=(VMEM_SPEC, VMEM_SPEC),
        scratch_shapes=[
            pltpu.VMEM((blocks * 3 * MOMENT_ROWS, LANES), F32),
            pltpu.VMEM((blocks, LANES), jnp.int32),
        ],
        cost_estimate=pl.CostEstimate(flops=1 << 28, bytes_accessed=1 << 16, transcendentals=0),
        compiler_params=pltpu.CompilerParams(vmem_limit_bytes=VMEM_LIMIT),
        name="sources",
    )(got.reshape(domains * SENT * quarters, LANES), cell_centers)
    others = [
        lax.ppermute(moments, "region", [(r, r ^ k) for r in range(regions)]) for k in range(1, regions)
    ]
    first, second = call(
        near_body,
        (pltpu.VMEM((FIRST_ROWS, count), F32), pltpu.VMEM((SECOND_ROWS, count), F32)),
        (near, target),
        1 << 32,
        "near",
    )
    rows = -(-(3 + 3 * (own // LANES)) // 8) * 8
    outgoing = call(
        functools.partial(force_body, regions),
        shape((domains, rows, LANES), F32),
        (midpoints, burgers, first, second, far, cell_hot, hot, *others),
        1 << 28,
        "force",
    )
    arrived = lax.all_to_all(outgoing, "domain", split_axis=0, concat_axis=0, tiled=True)
    return call(
        collect_body,
        (shape((3, 2 * count), F32), shape((3, own), F32)),
        (arrived,),
        1 << 12,
        "collect",
    )


def solution(mesh):
    both = ("region", "domain")
    in_specs = (P(None, both), P(None, both), P(None, both), P(both, None), P(None, both), P(both), P())
    out_specs = (P(None, both), P(None, both))
    return jax.shard_map(body, mesh=mesh, in_specs=in_specs, out_specs=out_specs, check_vma=False)
```

time: 187 us -> 46.3 us (0.25)
  blocking collectives: 84.1 us -> 11.5 us
  waiting for transfers between devices: 49.4 us -> 1.24 us
  matrix products: 21.4 us -> 0 us
  Pallas kernels: 0 us -> 15.9 us
  between operations: 14.3 us -> 0.75 us
  starting transfers between devices: 0.04 us -> 9.23 us
  other arithmetic: 7.69 us -> 0 us
  local copies, waits for them, and re-layouts: 9.35 us -> 7.09 us
    reduce_scatter x1 -> x0, waiting for transfers between devices: 49.4 us -> none  [body(): lax.psum_scatter(node_partial, 'domain', scatter_dimension=1, tiled=True)]
    psum x1 -> x0, blocking collectives: 38.9 us -> none  [body(): summed = lax.psum(partial_value, 'domain')]
    all_gather x2 -> x0, blocking collectives: 36.2 us -> none  [the longest x1 31 us: near_stress(): lax.all_gather(payload, 'domain', axis=1, tiled=True)]
    dot_general x26 -> x0, matrix products: 21.4 us -> none  [product(): jnp.dot(left, right, precision=EXACT, preferred_element_type=jnp.float32)]
    pallas_call x0 -> x6, Pallas kernels: none -> 15.9 us  [the longest x5 13.7 us: call(): pl.pallas_call(body, out_shape=out_shape, in_specs=[VMEM_SPEC] * len(inpu...]
    all_to_all x0 -> x1, starting transfers between devices: none -> 7.31 us  [body(): lax.all_to_all(payload, 'domain', split_axis=0, concat_axis=0, tiled=True)]
    scatter-add x2 -> x0, other arithmetic: 6.19 us -> none  [body(): node_partial.at[:, node_ids[0]].add(half).at[:, node_ids[1]].add(half)]
    all_to_all x1, blocking collectives: 9.02 us -> 11.5 us  [body(): lax.all_to_all(outgoing, 'domain', split_axis=0, concat_axis=0, tiled=True)]
  transfers between devices with their start and end apart: 1 -> 4, of which waited for: 1 -> 1; matrix products, arithmetic and copies ran while one was open for 2% -> 0% of each run, Pallas kernels for 0% -> 25%
where the time goes in v1:
time: 46.3 us; the launch traced here: 45.7 us
  Pallas kernels  15.9 us (34%)
  blocking collectives  11.5 us (25%)
  starting transfers between devices  9.23 us (20%)
  local copies, waits for them, and re-layouts  7.09 us (15%)
  waiting for transfers between devices  1.24 us (3%)
  between operations  0.75 us (2%)
    pallas_call x5, Pallas kernels, call(): pl.pallas_call(body, out_shape=out_shape, in_specs=[VMEM_SPEC] * len(inpu...  13.7 us
    all_to_all x1, blocking collectives, body(): lax.all_to_all(outgoing, 'domain', split_axis=0, concat_axis=0, tiled=True)  11.5 us
    all_to_all x1, starting transfers between devices, body(): lax.all_to_all(payload, 'domain', split_axis=0, concat_axis=0, tiled=True)  7.31 us
    unnamed x28, local copies, waits for them, and re-layouts  7.09 us
    pallas_call x1, Pallas kernels, body(): pl.pallas_call(functools.partial(source_body, regions), out_shape=(pltpu....  2.22 us
    ppermute x3, starting transfers between devices, body(): lax.ppermute(moments, 'region', [(r, r ^ k) for r in range(regions)])  1.92 us
    all_to_all x1, waiting for transfers between devices, body(): lax.all_to_all(payload, 'domain', split_axis=0, concat_axis=0, tiled=True)  1.23 us
  transfers between devices with their start and end apart: 4, of which 1 were waited for; matrix products, arithmetic and copies ran while one was open for 0% of the time, Pallas kernels for 25%

profile of v1, /device:TPU:0, one launch (start us, length us, event | category | flops | bytes accessed | tf_op | source)
XLA Modules:
  0.0 45.7 jit_solution(2159144205210629698)
XLA Ops:
  0.6 0.0 copy-start.2
  0.6 0.7 %copy-done.2 = f32[3,512]{1,0:T(4,128)S(1)} copy-done((f32[3,512]{1,0:T(4,128)S(1)}, f32[3,512]{1,0:T(4,128)}, u32[]{:S(2)}) %copy-start.2) | copy-done | bytes 6168
  1.3 0.7 %copy-done.5 = f32[3,512]{1,0:T(4,128)S(1)} copy-done((f32[3,512]{1,0:T(4,128)S(1)}, f32[3,512]{1,0:T(4,128)}, u32[]{:S(2)}) %copy-start.5) | copy-done | bytes 6168
  2.0 0.7 %copy-done.7 = f32[3,512]{1,0:T(4,128)S(1)} copy-done((f32[3,512]{1,0:T(4,128)S(1)}, f32[3,512]{1,0:T(4,128)}, u32[]{:S(2)}) %copy-start.7) | copy-done | bytes 6168
  2.7 0.7 %copy-done.8 = s32[512]{0:T(512)S(1)} copy-done((s32[512]{0:T(512)S(1)}, s32[512]{0:T(512)}, u32[]{:S(2)}) %copy-start.8) | copy-done | bytes 2072
  3.4 0.7 %pack.1 = f32[8,40,128]{2,1,0:T(8,128)} custom-call(f32[3,512]{1,0:T(4,128)S(1)} %copy-done.2, f32[3,512]{1,0:T(4,128)S(1)} %copy-done.7, f32[3,512]{1,0:T(4,128)S(1)} %copy-done.5, s32[1,512]{1,0:T(1,128)S(1)} %bitcast.4), custom_call_target="tpu_custom_call" | custom-call | flops 4096 | bytes 65536 | tf_op jit(solution)/shard_map/pack/pallas_call | solution.py:53
  4.1 7.3 %all-to-all-start = ((f32[8,40,128]{2,1,0:T(8,128)}), f32[8,40,128]{2,1,0:T(8,128)S(1)}, u32[]{:S(2)}, u32[]{:S(2)}) async-start(f32[8,40,128]{2,1,0:T(8,128)} %pack.1), calls=%async_computation | async-start | bytes 327680 | tf_op jit(solution)/shard_map/all_to_all | solution.py:292
  11.4 0.7 %copy-done.3 = f32[3,512]{1,0:T(4,128)S(1)} copy-done((f32[3,512]{1,0:T(4,128)S(1)}, f32[3,512]{1,0:T(4,128)}, u32[]{:S(2)}) %copy-start.3) | copy-done | bytes 6168
  12.1 0.7 %copy-done.9 = s32[512]{0:T(512)S(1)} copy-done((s32[512]{0:T(512)S(1)}, s32[512]{0:T(512)}, u32[]{:S(2)}) %copy-start.9) | copy-done | bytes 2072
  12.8 0.7 %copy-done.10 = f32[3,512]{1,0:T(4,128)S(1)} copy-done((f32[3,512]{1,0:T(4,128)S(1)}, f32[3,512]{1,0:T(4,128)}, u32[]{:S(2)}) %copy-start.10) | copy-done | bytes 6168
  13.5 0.7 %copy-done.12 = s32[2,512]{1,0:T(2,128)S(1)} copy-done((s32[2,512]{1,0:T(2,128)S(1)}, s32[2,512]{1,0:T(2,128)}, u32[]{:S(2)}) %copy-start.12) | copy-done | bytes 4120
  14.2 0.7 %copy-done.13 = s32[512,1]{0,1:T(1,128)S(1)} copy-done((s32[512,1]{0,1:T(1,128)S(1)}, s32[512,1]{0,1:T(1,128)}, u32[]{:S(2)}) %copy-start.13) | copy-done | bytes 2072
  14.8 2.0 %local.1 = (bf16[32,512]{1,0:T(8,128)(2,1)S(1)}, bf16[512,3072]{1,0:T(8,128)(2,1)S(1)}, bf16[128,512]{1,0:T(8,128)(2,1)S(1)}, bf16[1536,256]{1,0:T(8,128)(2,1)S(1)}) custom-call(f32[3,512]{1,0:T(4,128)S(1)} %copy-done.3, s32[1,512]{1,0:T(1,128)S(1)} %bitcast.6, s32[2,512]{1,0:T(2,128)S(1)} %copy-done.12, s32[1,512]{1,0:T(1,128)S(1)} %bitcast.5, ...), custom_call_target="tpu_custom_call" | custom-call | flops 1073741824 | bytes 65536 | tf_op jit(solution)/shard_map/local/pallas_call | solution.py:53
  16.9 0.9 %copy-done = bf16[1536,256]{1,0:T(8,128)(2,1)} copy-done((bf16[1536,256]{1,0:T(8,128)(2,1)}, bf16[1536,256]{1,0:T(8,128)(2,1)S(1)}, u32[]{:S(2)}) %copy-start) | copy-done | bytes 786456
  17.7 1.2 %all-to-all-done = f32[8,40,128]{2,1,0:T(8,128)S(1)} async-done(((f32[8,40,128]{2,1,0:T(8,128)}), f32[8,40,128]{2,1,0:T(8,128)S(1)}, u32[]{:S(2)}, u32[]{:S(2)}) %all-to-all-start) | async-done | bytes 163872 | tf_op jit(solution)/shard_map/all_to_all | solution.py:292
  19.0 2.2 %sources.1 = (f32[2560,128]{1,0:T(8,128)S(1)}, f32[32,128]{1,0:T(8,128)S(1)}) custom-call(f32[320,128]{1,0:T(8,128)S(1)} %bitcast.3, f32[3,512]{1,0:T(4,128)S(1)} %copy-done.11), custom_call_target="tpu_custom_call" | custom-call | flops 268435456 | bytes 65536 | tf_op jit(solution)/shard_map/sources/pallas_call | solution.py:307
  21.2 0.1 collective-permute-start
  21.3 1.6 %collective-permute-start.1 = (f32[32,128]{1,0:T(8,128)S(1)}, f32[32,128]{1,0:T(8,128)S(1)}, u32[]{:S(2)}, u32[]{:S(2)}) collective-permute-start(f32[32,128]{1,0:T(8,128)S(1)} %get-tuple-element.17), channel_id=1, source_target_pairs={{0,16},{8,24},{16,0},{24,8},{1,17},{9,25},{17,1},{25,9},{2,18},{10... | collective-permute-start | bytes 49160 | tf_op jit(solution)/shard_map/ppermute | solution.py:321
  22.8 0.3 collective-permute-start.2
  23.1 9.3 %near.1 = (f32[16,512]{1,0:T(8,128)S(1)}, f32[32,512]{1,0:T(8,128)S(1)}) custom-call(f32[2560,128]{1,0:T(8,128)S(1)} %get-tuple-element.10.near_ref, bf16[32,512]{1,0:T(8,128)(2,1)S(1)} %get-tuple-element.11.target_ref), custom_call_target="tpu_custom_call" | custom-call | flops 4294967296 | bytes 65536 | tf_op jit(solution)/shard_map/near/pallas_call | solution.py:53
  32.4 0.0 collective-permute-done.rest_0_
  32.5 1.1 %force.1 = f32[8,16,128]{2,1,0:T(8,128)S(1)} custom-call(f32[3,512]{1,0:T(4,128)S(1)} %copy-done.4, f32[3,512]{1,0:T(4,128)S(1)} %copy-done.6, f32[16,512]{1,0:T(8,128)S(1)} %get-tuple-element.12.first_ref, f32[32,512]{1,0:T(8,128)S(1)} %get-tuple-element.13.second_ref, bf16[1536,256]{1,0:T(8,128)(2,1)S(1)} %copy-done.1, ...), custom_call_target="tpu_custom_call" | custom-call | flops 268435456 | bytes 65536 | tf_op jit(solution)/shard_map/force/pallas_call | solution.py:53
  33.6 11.5 %all_to_all.10.got_ref = f32[8,16,128]{2,1,0:T(8,128)S(1)} all-to-all(f32[8,16,128]{2,1,0:T(8,128)S(1)} %force.1), channel_id=1, replica_groups=mesh['region'=4,'domain'=8] {'domain'}, dimensions={0} | all-to-all | bytes 131072 | tf_op jit(solution)/shard_map/all_to_all | solution.py:338
  45.1 0.6 %collect.1 = (f32[3,1024]{1,0:T(4,128)}, f32[3,256]{1,0:T(4,128)}) custom-call(f32[8,16,128]{2,1,0:T(8,128)S(1)} %all_to_all.10.got_ref), custom_call_target="tpu_custom_call" | custom-call | flops 4096 | bytes 65536 | tf_op jit(solution)/shard_map/collect/pallas_call | solution.py:53
  (19 shorter events, 0.0 us)
Async XLA Ops:
  0.6 0.7 %copy-start.2 = (f32[3,512]{1,0:T(4,128)S(1)}, f32[3,512]{1,0:T(4,128)}, u32[]{:S(2)}) copy-start(f32[3,512]{1,0:T(4,128)} %m_ref.5) | copy-start | bytes 18436
  1.3 0.7 %copy-start.5 = (f32[3,512]{1,0:T(4,128)S(1)}, f32[3,512]{1,0:T(4,128)}, u32[]{:S(2)}) copy-start(f32[3,512]{1,0:T(4,128)} %b_ref.3) | copy-start | bytes 18436
  2.0 0.7 %copy-start.7 = (f32[3,512]{1,0:T(4,128)S(1)}, f32[3,512]{1,0:T(4,128)}, u32[]{:S(2)}) copy-start(f32[3,512]{1,0:T(4,128)} %l_ref.1) | copy-start | bytes 18436
  2.7 0.7 %copy-start.8 = (s32[512]{0:T(512)S(1)}, s32[512]{0:T(512)}, u32[]{:S(2)}) copy-start(s32[512]{0:T(512)} %param.12) | copy-start | bytes 6148
  3.4 15.6 %copy-start.11 = (f32[3,512]{1,0:T(4,128)S(1)}, f32[3,512]{1,0:T(4,128)}, u32[]{:S(2)}) copy-start(f32[3,512]{1,0:T(4,128)} %centers_ref.3) | copy-start | bytes 18436
  4.1 14.9 %all-to-all-start = ((f32[8,40,128]{2,1,0:T(8,128)}), f32[8,40,128]{2,1,0:T(8,128)S(1)}, u32[]{:S(2)}, u32[]{:S(2)}) async-start(f32[8,40,128]{2,1,0:T(8,128)} %pack.1), calls=%async_computation | async-start | bytes 327680 | tf_op jit(solution)/shard_map/all_to_all | solution.py:292
  11.4 0.7 %copy-start.3 = (f32[3,512]{1,0:T(4,128)S(1)}, f32[3,512]{1,0:T(4,128)}, u32[]{:S(2)}) copy-start(f32[3,512]{1,0:T(4,128)} %m_ref.5) | copy-start | bytes 18436
  12.1 0.7 %copy-start.9 = (s32[512]{0:T(512)S(1)}, s32[512]{0:T(512)}, u32[]{:S(2)}) copy-start(s32[512]{0:T(512)} %param.12) | copy-start | bytes 6148
  12.8 0.7 %copy-start.10 = (f32[3,512]{1,0:T(4,128)S(1)}, f32[3,512]{1,0:T(4,128)}, u32[]{:S(2)}) copy-start(f32[3,512]{1,0:T(4,128)} %centers_ref.3) | copy-start | bytes 18436
  13.5 0.7 %copy-start.12 = (s32[2,512]{1,0:T(2,128)S(1)}, s32[2,512]{1,0:T(2,128)}, u32[]{:S(2)}) copy-start(s32[2,512]{1,0:T(2,128)} %nodes_ref.1) | copy-start | bytes 12292
  14.2 0.7 %copy-start.13 = (s32[512,1]{0,1:T(1,128)S(1)}, s32[512,1]{0,1:T(1,128)}, u32[]{:S(2)}) copy-start(s32[512,1]{0,1:T(1,128)} %param.10) | copy-start | bytes 6148
  16.8 0.9 %copy-start = (bf16[1536,256]{1,0:T(8,128)(2,1)}, bf16[1536,256]{1,0:T(8,128)(2,1)S(1)}, u32[]{:S(2)}) copy-start(bf16[1536,256]{1,0:T(8,128)(2,1)S(1)} %get-tuple-element.14.far_ref) | copy-start | bytes 2359300
  21.2 11.2 %collective-permute-start = (f32[32,128]{1,0:T(8,128)S(1)}, f32[32,128]{1,0:T(8,128)S(1)}, u32[]{:S(2)}, u32[]{:S(2)}) collective-permute-start(f32[32,128]{1,0:T(8,128)S(1)} %get-tuple-element.17), channel_id=1, source_target_pairs={{0,8},{8,0},{16,24},{24,16},{1,9},{9,1},{17,25},{25,17},{2,10},{10... | collective-permute-start | bytes 49160 | tf_op jit(solution)/shard_map/ppermute | solution.py:321
  21.3 11.2 %collective-permute-start.1 = (f32[32,128]{1,0:T(8,128)S(1)}, f32[32,128]{1,0:T(8,128)S(1)}, u32[]{:S(2)}, u32[]{:S(2)}) collective-permute-start(f32[32,128]{1,0:T(8,128)S(1)} %get-tuple-element.17), channel_id=1, source_target_pairs={{0,16},{8,24},{16,0},{24,8},{1,17},{9,25},{17,1},{25,9},{2,18},{10... | collective-permute-start | bytes 49160 | tf_op jit(solution)/shard_map/ppermute | solution.py:321
  22.8 9.6 %collective-permute-start.2 = (f32[32,128]{1,0:T(8,128)S(1)}, f32[32,128]{1,0:T(8,128)S(1)}, u32[]{:S(2)}, u32[]{:S(2)}) collective-permute-start(f32[32,128]{1,0:T(8,128)S(1)} %get-tuple-element.17), channel_id=1, source_target_pairs={{0,24},{8,16},{16,8},{24,0},{1,25},{9,17},{17,9},{25,1},{2,26},{10... | collective-permute-start | bytes 49160 | tf_op jit(solution)/shard_map/ppermute | solution.py:321
  23.1 9.3 %copy-start.1 = (bf16[1536,256]{1,0:T(8,128)(2,1)S(1)}, bf16[1536,256]{1,0:T(8,128)(2,1)}, u32[]{:S(2)}) copy-start(bf16[1536,256]{1,0:T(8,128)(2,1)} %copy-done) | copy-start | bytes 2359300
  23.1 9.3 %copy-start.4 = (f32[3,512]{1,0:T(4,128)S(1)}, f32[3,512]{1,0:T(4,128)}, u32[]{:S(2)}) copy-start(f32[3,512]{1,0:T(4,128)} %m_ref.5) | copy-start | bytes 18436
  23.1 9.3 %copy-start.6 = (f32[3,512]{1,0:T(4,128)S(1)}, f32[3,512]{1,0:T(4,128)}, u32[]{:S(2)}) copy-start(f32[3,512]{1,0:T(4,128)} %b_ref.3) | copy-start | bytes 18436

commit v2 on v1

--- a/solution.py
+++ b/solution.py
@@ -13,10 +13,12 @@
 BF16 = jnp.bfloat16
 SYM = ((0, 0), (1, 1), (2, 2), (0, 1), (0, 2), (1, 2))
 SENT = 10
-DIST_ROWS, FIRST_ROWS, SECOND_ROWS = 32, 16, 32
-NEAR_ROWS = DIST_ROWS + FIRST_ROWS + SECOND_ROWS
+SOURCE_ROWS = 24
+DIST_ROWS = 48
+FIRST_ROWS, SECOND_ROWS = 16, 32
+PIPELINE = 16
 MOMENT_ROWS = 32
-VMEM_LIMIT = 32 << 20
+VMEM_LIMIT = 16 << 20
 VMEM_SPEC = pl.BlockSpec(memory_space=pltpu.VMEM)
 
 
@@ -49,19 +51,37 @@
     return ((region.astype(F32) + 0.5) / regions, 0.5, 0.5)
 
 
-def call(body, out_shape, inputs, flops, name):
+def call(body, out_shape, inputs, flops, name, scratch=(), fetched=()):
+    space = pl.BlockSpec(memory_space=pltpu.HBM) if fetched else VMEM_SPEC
+    if fetched:
+        inputs = [pltpu.with_memory_space_constraint(x, pltpu.HBM) for x in inputs]
+    scratch = list(scratch) + [pltpu.VMEM(x.shape, x.dtype) for x in fetched]
+    if fetched:
+        scratch.append(pltpu.SemaphoreType.DMA((len(fetched),)))
     return pl.pallas_call(
         body,
         out_shape=out_shape,
-        in_specs=[VMEM_SPEC] * len(inputs),
+        in_specs=[space] * len(inputs),
         out_specs=jax.tree.map(lambda _: VMEM_SPEC, out_shape),
+        scratch_shapes=scratch,
         cost_estimate=pl.CostEstimate(flops=flops, bytes_accessed=1 << 16, transcendentals=0),
         compiler_params=pltpu.CompilerParams(vmem_limit_bytes=VMEM_LIMIT),
         name=name,
     )(*inputs)
 
 
-def pack_body(m_ref, l_ref, b_ref, cell_ref, out_ref):
+def fetch(sources, buffers, semaphores):
+    copies = [pltpu.make_async_copy(s, t, semaphores.at[i]) for i, (s, t) in enumerate(zip(sources, buffers))]
+    for copy in copies:
+        copy.start()
+    for copy in copies:
+        copy.wait()
+
+
+def pack_body(*refs):
+    sources, out_ref, buffers, semaphores = refs[:4], refs[4], refs[5:9], refs[9]
+    fetch(sources, buffers, semaphores)
+    m_ref, l_ref, b_ref, cell_ref = buffers
     quarters = m_ref.shape[1] // LANES
     parts = [ref[...] for ref in (m_ref, l_ref, b_ref)] + [cell_ref[...].astype(F32)]
     rows = [
@@ -75,7 +95,11 @@
         out_ref[d] = block
 
 
-def local_body(regions, domains, m_ref, dest_ref, nodes_ref, cell_ref, centers_ref, target_ref, hot_ref, cell_hot_ref, far_ref):
+def local_body(regions, domains, *refs):
+    sources, outputs, buffers, semaphores = refs[:5], refs[5:9], refs[9:14], refs[14]
+    fetch(sources, buffers, semaphores)
+    m_ref, dest_ref, nodes_ref, cell_ref, centers_ref = buffers
+    target_ref, hot_ref, cell_hot_ref, far_ref = outputs
     count = m_ref.shape[1]
     cells = centers_ref.shape[1] // regions
     region = lax.axis_index("region")
@@ -83,9 +107,10 @@
     x = [m_ref[a : a + 1, :] - middle[a] for a in range(3)]
     parts = [split3(-2.0 * v) for v in x]
     norm = split3(x[0] * x[0] + x[1] * x[1] + x[2] * x[2] + CORE2)
-    ones = jnp.ones((1, count), F32)
-    rows = [parts[a][p] for a in range(3) for p in (0, 1, 2, 0, 1, 0)]
-    rows += [ones, ones, ones] + list(norm) + [jnp.zeros((DIST_ROWS - 24, count), F32)]
+    one, none, pad = jnp.ones((1, count), F32), jnp.zeros((1, count), F32), jnp.zeros((3, count), F32)
+    rows = []
+    for p, of_source, of_target in ((0, one, norm[0]), (1, none, norm[1]), (2, none, norm[2]), (0, one, none), (1, none, none), (0, one, none)):
+        rows += [parts[0][p], parts[1][p], parts[2][p], of_source, of_target, pad]
     target_ref[...] = jnp.concatenate(rows, axis=0).astype(BF16)
     dest = dest_ref[...]
     hot = (lax.broadcasted_iota(jnp.int32, (domains, count), 0) == dest).astype(BF16)
@@ -123,14 +148,14 @@
             far_ref[row : row + cells, cells : 2 * cells] = low.astype(BF16)
 
 
-def source_body(regions, got_ref, centers_ref, near_ref, moment_ref, terms_ref, cell_rows_ref):
-    sent_rows = SENT * 4
+def source_body(regions, got_ref, centers_ref, near_ref, moment_ref):
+    quarters = 4
+    sent_rows = SENT * quarters
     devices = got_ref.shape[0] // sent_rows
     cells = moment_ref.shape[1]
     middle = middle_of(regions)
     zero = jnp.zeros((8, LANES), F32)
     one = jnp.ones((8, LANES), F32)
-    quarters = 4
     for group in range(devices // 8):
         for quarter in range(quarters):
 
@@ -143,43 +168,32 @@
             b = [value(6 + a) for a in range(3)]
             q = [b[1] * l[2] - b[2] * l[1], b[2] * l[0] - b[0] * l[2], b[0] * l[1] - b[1] * l[0]]
             outer = [b[i] * l[i] if i == j else 0.5 * (b[i] * l[j] + b[j] * l[i]) for i, j in SYM]
-            second = q + [q[i] * m[i] if i == j else 0.5 * (q[i] * m[j] + q[j] * m[i]) for i, j in SYM]
-            parts = [split3(v) for v in m]
-            norm = split3(m[0] * m[0] + m[1] * m[1] + m[2] * m[2])
-            rows = [parts[a][p] for a in range(3) for p in (0, 0, 0, 1, 1, 2)]
-            rows += list(norm) + [one, one, one] + [zero] * (DIST_ROWS - 24)
-            pair = [split2(v) for v in outer]
-            for p in range(2):
-                rows += [v[p] for v in pair] + [None] * (FIRST_ROWS // 2 - 6)
-            pair = [split2(v) for v in second]
-            for p in range(2):
-                rows += [v[p] for v in pair] + [None] * (SECOND_ROWS // 2 - 9)
+            second = [q[i] * m[i] if i == j else 0.5 * (q[i] * m[j] + q[j] * m[i]) for i, j in SYM]
+            norm = m[0] * m[0] + m[1] * m[1] + m[2] * m[2]
+            rows = m + [norm, one, value(9), zero, zero] + outer + q + second + [zero]
             for f, row in enumerate(rows):
-                near_ref[pl.ds(first_block * NEAR_ROWS + f, 8, stride=NEAR_ROWS), :] = zero if row is None else row
-            terms = outer + [q[0], q[1]]
-            for a in range(3):
-                terms += [v * m[a] for v in outer] + ([q[2], zero] if a == 0 else [zero, zero])
-            terms = [split3(v) for v in terms]
-            for p in range(3):
-                for f, row in enumerate(terms):
-                    at = first_block * 3 * MOMENT_ROWS + p * MOMENT_ROWS + f
-                    terms_ref[pl.ds(at, 8, stride=3 * MOMENT_ROWS), :] = row[p]
-            cell_rows_ref[first_block : first_block + 8, :] = value(9).astype(jnp.int32)
+                near_ref[pl.ds(first_block * SOURCE_ROWS + f, 8, stride=SOURCE_ROWS), :] = row
 
     def step(i, total):
-        left = [terms_ref[pl.ds(pl.multiple_of((2 * i + h) * 3 * MOMENT_ROWS, 8), 3 * MOMENT_ROWS), :] for h in range(2)]
+        left, rows = [], []
+        for h in range(2):
+            part = near_ref[pl.ds(pl.multiple_of((2 * i + h) * SOURCE_ROWS, 8), SOURCE_ROWS), :]
+            plain = part[8:16]
+            terms = [split3(v) for v in [plain] + [plain * part[a : a + 1] for a in range(3)] + [part[16:24]]]
+            left.append(jnp.concatenate([t[p] for p in range(3) for t in terms], axis=0))
+            rows.append(part[5:6])
         left = jnp.concatenate(left, axis=1).astype(BF16)
-        rows = [cell_rows_ref[pl.ds(2 * i + h, 1), :] for h in range(2)]
-        hot = jnp.concatenate(rows, axis=1) == lax.broadcasted_iota(jnp.int32, (cells, 2 * LANES), 0)
+        row = jnp.concatenate(rows, axis=1).astype(jnp.int32)
+        hot = row == lax.broadcasted_iota(jnp.int32, (cells, 2 * LANES), 0)
         return total + dot_nt(left, hot.astype(BF16))
 
     blocks = devices * quarters
-    total = lax.fori_loop(0, blocks // 2, step, jnp.zeros((3 * MOMENT_ROWS, cells), F32), unroll=4)
-    total = total[0:32] + total[32:64] + total[64:96]
+    total = lax.fori_loop(0, blocks // 2, step, jnp.zeros((120, cells), F32), unroll=4)
+    total = total[0:40] + total[40:80] + total[80:120]
     region = lax.axis_index("region")
     here = centers_ref[:, pl.ds(pl.multiple_of(region * cells, cells), cells)]
     charge = total[0:6]
-    n = [total[6:7], total[7:8], total[14:15]]
+    n = [total[6:7], total[7:8], total[32:33]]
     none = jnp.zeros((1, cells), F32)
     fold = [
         [n[0], none, none, 0.5 * n[1], 0.5 * n[2], none],
@@ -194,29 +208,57 @@
         moment_ref[8 + 8 * a : 16 + 8 * a, :] = jnp.concatenate([about, pad], axis=0)
 
 
-def near_body(near_ref, target_ref, first_ref, second_ref):
-    blocks = near_ref.shape[0] // NEAR_ROWS
-    count = target_ref.shape[1]
+def near_body(near_ref, target_ref, first_ref, second_ref, *scratch):
+    squares, factors = scratch[0:2], scratch[2:4]
+    steps = near_ref.shape[0] // SOURCE_ROWS // 2
     first_ref[...] = jnp.zeros_like(first_ref)
     second_ref[...] = jnp.zeros_like(second_ref)
 
-    def step(i, carry):
-        part = [near_ref[pl.ds(pl.multiple_of((2 * i + h) * NEAR_ROWS, 8), NEAR_ROWS), :] for h in range(2)]
-        factors = jnp.concatenate([jnp.transpose(p[0:DIST_ROWS]) for p in part], axis=0).astype(BF16)
-        rows = jnp.concatenate([p[DIST_ROWS:] for p in part], axis=1).astype(BF16)
-        for start in range(0, count, 256):
-            at = slice(start, start + 256)
-            g1 = lax.rsqrt(dot(factors, target_ref[:, at]))
-            g3 = g1 * g1 * g1
-            high = g1.astype(BF16)
-            low = (g1 - high.astype(F32)).astype(BF16)
-            first_ref[:, at] += dot(rows[0:FIRST_ROWS], high) + dot(rows[0:FIRST_ROWS], low)
-            high = g3.astype(BF16)
-            low = (g3 - high.astype(F32)).astype(BF16)
-            second_ref[:, at] += dot(rows[FIRST_ROWS:], high) + dot(rows[FIRST_ROWS:], low)
-        return carry
-
-    lax.fori_loop(0, blocks // 2, step, 0, unroll=2)
+    def rows_of(step, start, size):
+        at = [(2 * step + h) * SOURCE_ROWS + start for h in range(2)]
+        return [near_ref[pl.ds(i if isinstance(i, int) else pl.multiple_of(i, 8), size), :] for i in at]
+
+    def distances(step, slot):
+        left = []
+        for part in rows_of(step, 0, 8):
+            p = split3(part)
+            left.append(jnp.transpose(jnp.concatenate([p[0], p[0], p[0], p[1], p[1], p[2]], axis=0)))
+        squares[slot][...] = dot(jnp.concatenate(left, axis=0).astype(BF16), target_ref[...])
+
+    def powers(slot):
+        g1 = lax.rsqrt(squares[slot][...])
+        for k, g in ((0, g1), (2, g1 * g1 * g1)):
+            high = g.astype(BF16)
+            factors[slot][k] = high
+            factors[slot][k + 1] = (g - high.astype(F32)).astype(BF16)
+
+    def products(step, slot):
+        high, low = split2(jnp.concatenate(rows_of(step, 8, 16), axis=1))
+        left = jnp.concatenate([high[0:8], low[0:8]], axis=0).astype(BF16)
+        first_ref[...] += dot(left, factors[slot][0]) + dot(left, factors[slot][1])
+        left = jnp.concatenate([high, low], axis=0).astype(BF16)
+        second_ref[...] += dot(left, factors[slot][2]) + dot(left, factors[slot][3])
+
+    def pipeline(first, length):
+        distances(first, 0)
+        distances(first + 1, 1)
+        powers(0)
+        for t in range(length):
+            if t + 2 < length:
+                distances(first + t + 2, t % 2)
+            if t + 1 < length:
+                powers((t + 1) % 2)
+            products(first + t, t % 2)
+
+    if steps <= PIPELINE:
+        pipeline(0, steps)
+    else:
+
+        def part(i, carry):
+            pipeline(i * PIPELINE, PIPELINE)
+            return carry
+
+        lax.fori_loop(0, steps // PIPELINE, part, 0)
 
 
 def stacked3(x):
@@ -239,9 +281,9 @@
     second = second_ref[...]
     second = second[0:16] + second[16:32]
     x = [m_ref[a : a + 1, :] - middle[a] for a in range(3)]
-    q = [second[a : a + 1] for a in range(3)]
+    q = [second[6 + a : 7 + a] for a in range(3)]
     cross = [q[i] * x[i] if i == j else 0.5 * (q[i] * x[j] + q[j] * x[i]) for i, j in SYM]
-    sigma = first[0:6] + first[8:14] + (jnp.concatenate(cross, axis=0) - second[3:9]) + field[0:6]
+    sigma = first[0:6] + first[8:14] + (jnp.concatenate(cross, axis=0) - second[9:15]) + field[0:6]
     at = {}
     for row, (i, j) in enumerate(SYM):
         at[i, j] = at[j, i] = sigma[row : row + 1]
@@ -282,15 +324,13 @@
     dest_row = destination.reshape(1, count)
     shape = jax.ShapeDtypeStruct
     quarters = count // LANES
+    inputs = (midpoints, line_vectors, burgers, cell_row)
     payload = call(
-        pack_body,
-        shape((domains, SENT * quarters, LANES), F32),
-        (midpoints, line_vectors, burgers, cell_row),
-        1 << 12,
-        "pack",
+        pack_body, shape((domains, SENT * quarters, LANES), F32), inputs, 1 << 12, "pack", fetched=inputs
     )
     got = lax.all_to_all(payload, "domain", split_axis=0, concat_axis=0, tiled=True)
     far_rows = (regions - 1) * 4 * cells
+    inputs = (midpoints, dest_row, node_ids, cell_row, cell_centers)
     target, hot, cell_hot, far = call(
         functools.partial(local_body, regions, domains),
         (
@@ -299,24 +339,19 @@
             pltpu.VMEM((cells, count), BF16),
             pltpu.VMEM((far_rows, 2 * cells), BF16),
         ),
-        (midpoints, dest_row, node_ids, cell_row, cell_centers),
+        inputs,
         1 << 30,
         "local",
+        fetched=inputs,
     )
     blocks = domains * quarters
-    near, moments = pl.pallas_call(
+    near, moments = call(
         functools.partial(source_body, regions),
-        out_shape=(pltpu.VMEM((blocks * NEAR_ROWS, LANES), F32), shape((MOMENT_ROWS, cells), F32)),
-        in_specs=[VMEM_SPEC] * 2,
-        out_specs=(VMEM_SPEC, VMEM_SPEC),
-        scratch_shapes=[
-            pltpu.VMEM((blocks * 3 * MOMENT_ROWS, LANES), F32),
-            pltpu.VMEM((blocks, LANES), jnp.int32),
-        ],
-        cost_estimate=pl.CostEstimate(flops=1 << 28, bytes_accessed=1 << 16, transcendentals=0),
-        compiler_params=pltpu.CompilerParams(vmem_limit_bytes=VMEM_LIMIT),
-        name="sources",
-    )(got.reshape(domains * SENT * quarters, LANES), cell_centers)
+        (pltpu.VMEM((blocks * SOURCE_ROWS, LANES), F32), shape((MOMENT_ROWS, cells), F32)),
+        (got.reshape(domains * SENT * quarters, LANES), cell_centers),
+        1 << 28,
+        "sources",
+    )
     others = [
         lax.ppermute(moments, "region", [(r, r ^ k) for r in range(regions)]) for k in range(1, regions)
     ]
@@ -326,6 +361,7 @@
         (near, target),
         1 << 32,
         "near",
+        scratch=[pltpu.VMEM((2 * LANES, count), F32)] * 2 + [pltpu.VMEM((4, 2 * LANES, count), BF16)] * 2,
     )
     rows = -(-(3 + 3 * (own // LANES)) // 8) * 8
     outgoing = call(

time: 46.3 us -> 35.8 us (0.77)
  local copies, waits for them, and re-layouts: 7.09 us -> 0.9 us
  Pallas kernels: 15.9 us -> 11.2 us
  waiting for transfers between devices: 1.24 us -> 3.87 us
  blocking collectives: 11.5 us -> 9.56 us
    unnamed x28 -> x10, local copies, waits for them, and re-layouts: 7.09 us -> 0.9 us
    pallas_call x6, Pallas kernels: 15.9 us -> 11.2 us  [call(): pl.pallas_call(body, out_shape=out_shape, in_specs=[space] * len(inputs),...]
    all_to_all x1, waiting for transfers between devices: 1.23 us -> 3.86 us  [body(): lax.all_to_all(payload, 'domain', split_axis=0, concat_axis=0, tiled=True)]
    all_to_all x1, blocking collectives: 11.5 us -> 9.56 us  [body(): lax.all_to_all(outgoing, 'domain', split_axis=0, concat_axis=0, tiled=True)]
  transfers between devices with their start and end apart: 4 -> 4, of which waited for: 1 -> 1; matrix products, arithmetic and copies ran while one was open for 0% -> 0% of each run, Pallas kernels for 25% -> 19%
where the time goes in v2:
time: 35.8 us; the launch traced here: 35.5 us
  Pallas kernels  11.2 us (31%)
  blocking collectives  9.56 us (27%)
  starting transfers between devices  9.24 us (26%)
  waiting for transfers between devices  3.87 us (11%)
  local copies, waits for them, and re-layouts  0.9 us (3%)
  between operations  0.74 us (2%)
    pallas_call x6, Pallas kernels, call(): pl.pallas_call(body, out_shape=out_shape, in_specs=[space] * len(inputs),...  11.2 us
    all_to_all x1, blocking collectives, body(): lax.all_to_all(outgoing, 'domain', split_axis=0, concat_axis=0, tiled=True)  9.56 us
    all_to_all x1, starting transfers between devices, body(): lax.all_to_all(payload, 'domain', split_axis=0, concat_axis=0, tiled=True)  7.32 us
    all_to_all x1, waiting for transfers between devices, body(): lax.all_to_all(payload, 'domain', split_axis=0, concat_axis=0, tiled=True)  3.86 us
    ppermute x3, starting transfers between devices, body(): lax.ppermute(moments, 'region', [(r, r ^ k) for r in range(regions)])  1.92 us
    unnamed x10, local copies, waits for them, and re-layouts  0.9 us
  transfers between devices with their start and end apart: 4, of which 1 were waited for; matrix products, arithmetic and copies ran while one was open for 0% of the time, Pallas kernels for 19%

profile of v2, /device:TPU:0, one launch (start us, length us, event | category | flops | bytes accessed | tf_op | source)
XLA Modules:
  0.0 35.5 jit_solution(1734052521352813929)
XLA Ops:
  0.6 0.0 copy-start.4
  0.6 1.4 %pack.1 = f32[8,40,128]{2,1,0:T(8,128)} custom-call(f32[3,512]{1,0:T(4,128)} %m_ref.1, f32[3,512]{1,0:T(4,128)} %refs_1_.1, f32[3,512]{1,0:T(4,128)} %b_ref.1, s32[1,512]{1,0:T(1,128)} %bitcast.4), custom_call_target="tpu_custom_call" | custom-call | flops 4096 | bytes 65536 | tf_op jit(solution)/shard_map/pack/pallas_call | solution.py:61
  2.1 7.3 %all-to-all-start = ((f32[8,40,128]{2,1,0:T(8,128)}), f32[8,40,128]{2,1,0:T(8,128)S(1)}, u32[]{:S(2)}, u32[]{:S(2)}) async-start(f32[8,40,128]{2,1,0:T(8,128)} %pack.1), calls=%async_computation | async-start | bytes 327680 | tf_op jit(solution)/shard_map/all_to_all | solution.py:331
  9.4 2.8 %local.1 = (bf16[48,512]{1,0:T(8,128)(2,1)S(1)}, bf16[512,3072]{1,0:T(8,128)(2,1)S(1)}, bf16[128,512]{1,0:T(8,128)(2,1)S(1)}, bf16[1536,256]{1,0:T(8,128)(2,1)S(1)}) custom-call(f32[3,512]{1,0:T(4,128)} %m_ref.1, s32[1,512]{1,0:T(1,128)} %bitcast.6, s32[2,512]{1,0:T(2,128)} %refs_2_.3, s32[1,512]{1,0:T(1,128)} %bitcast.5, f32[3,512]{1,0:T(4,128)} %refs_4_.1), custom_call_target="tpu_custom_call" | custom-call | flops 1073741824 | bytes 65536 | tf_op jit(solution)/shard_map/local/pallas_call | solution.py:61
  12.2 0.0 copy-start
  12.2 0.9 %copy-done = bf16[1536,256]{1,0:T(8,128)(2,1)} copy-done((bf16[1536,256]{1,0:T(8,128)(2,1)}, bf16[1536,256]{1,0:T(8,128)(2,1)S(1)}, u32[]{:S(2)}) %copy-start) | copy-done | bytes 786456
  13.1 3.9 %all-to-all-done = f32[8,40,128]{2,1,0:T(8,128)S(1)} async-done(((f32[8,40,128]{2,1,0:T(8,128)}), f32[8,40,128]{2,1,0:T(8,128)S(1)}, u32[]{:S(2)}, u32[]{:S(2)}) %all-to-all-start) | async-done | bytes 163872 | tf_op jit(solution)/shard_map/all_to_all | solution.py:331
  17.0 0.0 copy-done.4
  17.0 1.1 %sources.1 = (f32[768,128]{1,0:T(8,128)S(1)}, f32[32,128]{1,0:T(8,128)S(1)}) custom-call(f32[320,128]{1,0:T(8,128)S(1)} %bitcast.3, f32[3,512]{1,0:T(4,128)S(1)} %copy-done.4), custom_call_target="tpu_custom_call" | custom-call | flops 268435456 | bytes 65536 | tf_op jit(solution)/shard_map/sources/pallas_call | solution.py:61
  18.1 0.1 collective-permute-start
  18.2 1.6 %collective-permute-start.1 = (f32[32,128]{1,0:T(8,128)S(1)}, f32[32,128]{1,0:T(8,128)S(1)}, u32[]{:S(2)}, u32[]{:S(2)}) collective-permute-start(f32[32,128]{1,0:T(8,128)S(1)} %get-tuple-element.17), channel_id=1, source_target_pairs={{0,16},{8,24},{16,0},{24,8},{1,17},{9,25},{17,1},{25,9},{2,18},{10... | collective-permute-start | bytes 49160 | tf_op jit(solution)/shard_map/ppermute | solution.py:356
  19.8 0.3 collective-permute-start.2
  20.1 0.0 copy-start.1
  20.1 0.0 copy-start.2
  20.1 4.0 %near.1 = (f32[16,512]{1,0:T(8,128)S(1)}, f32[32,512]{1,0:T(8,128)S(1)}) custom-call(f32[768,128]{1,0:T(8,128)S(1)} %get-tuple-element.10.near_ref, bf16[48,512]{1,0:T(8,128)(2,1)S(1)} %get-tuple-element.11.target_ref), custom_call_target="tpu_custom_call" | custom-call | flops 4294967296 | bytes 65536 | tf_op jit(solution)/shard_map/near/pallas_call | solution.py:61
  24.1 0.0 collective-permute-done.rest_0_
  24.1 0.0 collective-permute-done.1.rest_1_
  24.1 0.0 collective-permute-done.2.rest_2_
  24.1 0.0 copy-done.1
  24.1 0.0 copy-done.2
  24.1 0.0 copy-done.3
  24.2 1.1 %force.1 = f32[8,16,128]{2,1,0:T(8,128)S(1)} custom-call(f32[3,512]{1,0:T(4,128)S(1)} %copy-done.2, f32[3,512]{1,0:T(4,128)S(1)} %copy-done.3, f32[16,512]{1,0:T(8,128)S(1)} %get-tuple-element.12.first_ref, f32[32,512]{1,0:T(8,128)S(1)} %get-tuple-element.13.second_ref, bf16[1536,256]{1,0:T(8,128)(2,1)S(1)} %copy-done.1, ...), custom_call_target="tpu_custom_call" | custom-call | flops 268435456 | bytes 65536 | tf_op jit(solution)/shard_map/force/pallas_call | solution.py:61
  25.3 9.6 %all_to_all.10.got_ref = f32[8,16,128]{2,1,0:T(8,128)S(1)} all-to-all(f32[8,16,128]{2,1,0:T(8,128)S(1)} %force.1), channel_id=1, replica_groups=mesh['region'=4,'domain'=8] {'domain'}, dimensions={0} | all-to-all | bytes 131072 | tf_op jit(solution)/shard_map/all_to_all | solution.py:374
  34.9 0.6 %collect.1 = (f32[3,1024]{1,0:T(4,128)}, f32[3,256]{1,0:T(4,128)}) custom-call(f32[8,16,128]{2,1,0:T(8,128)S(1)} %all_to_all.10.got_ref), custom_call_target="tpu_custom_call" | custom-call | flops 4096 | bytes 65536 | tf_op jit(solution)/shard_map/collect/pallas_call | solution.py:61
  (1 shorter events, 0.0 us)
Async XLA Ops:
  0.6 16.4 %copy-start.4 = (f32[3,512]{1,0:T(4,128)S(1)}, f32[3,512]{1,0:T(4,128)}, u32[]{:S(2)}) copy-start(f32[3,512]{1,0:T(4,128)} %refs_4_.1) | copy-start | bytes 18436
  2.1 14.9 %all-to-all-start = ((f32[8,40,128]{2,1,0:T(8,128)}), f32[8,40,128]{2,1,0:T(8,128)S(1)}, u32[]{:S(2)}, u32[]{:S(2)}) async-start(f32[8,40,128]{2,1,0:T(8,128)} %pack.1), calls=%async_computation | async-start | bytes 327680 | tf_op jit(solution)/shard_map/all_to_all | solution.py:331
  12.2 0.9 %copy-start = (bf16[1536,256]{1,0:T(8,128)(2,1)}, bf16[1536,256]{1,0:T(8,128)(2,1)S(1)}, u32[]{:S(2)}) copy-start(bf16[1536,256]{1,0:T(8,128)(2,1)S(1)} %get-tuple-element.14.far_ref) | copy-start | bytes 2359300
  18.1 6.0 %collective-permute-start = (f32[32,128]{1,0:T(8,128)S(1)}, f32[32,128]{1,0:T(8,128)S(1)}, u32[]{:S(2)}, u32[]{:S(2)}) collective-permute-start(f32[32,128]{1,0:T(8,128)S(1)} %get-tuple-element.17), channel_id=1, source_target_pairs={{0,8},{8,0},{16,24},{24,16},{1,9},{9,1},{17,25},{25,17},{2,10},{10... | collective-permute-start | bytes 49160 | tf_op jit(solution)/shard_map/ppermute | solution.py:356
  18.2 5.9 %collective-permute-start.1 = (f32[32,128]{1,0:T(8,128)S(1)}, f32[32,128]{1,0:T(8,128)S(1)}, u32[]{:S(2)}, u32[]{:S(2)}) collective-permute-start(f32[32,128]{1,0:T(8,128)S(1)} %get-tuple-element.17), channel_id=1, source_target_pairs={{0,16},{8,24},{16,0},{24,8},{1,17},{9,25},{17,1},{25,9},{2,18},{10... | collective-permute-start | bytes 49160 | tf_op jit(solution)/shard_map/ppermute | solution.py:356
  19.8 4.4 %collective-permute-start.2 = (f32[32,128]{1,0:T(8,128)S(1)}, f32[32,128]{1,0:T(8,128)S(1)}, u32[]{:S(2)}, u32[]{:S(2)}) collective-permute-start(f32[32,128]{1,0:T(8,128)S(1)} %get-tuple-element.17), channel_id=1, source_target_pairs={{0,24},{8,16},{16,8},{24,0},{1,25},{9,17},{17,9},{25,1},{2,26},{10... | collective-permute-start | bytes 49160 | tf_op jit(solution)/shard_map/ppermute | solution.py:356
  20.1 4.1 %copy-start.1 = (bf16[1536,256]{1,0:T(8,128)(2,1)S(1)}, bf16[1536,256]{1,0:T(8,128)(2,1)}, u32[]{:S(2)}) copy-start(bf16[1536,256]{1,0:T(8,128)(2,1)} %copy-done) | copy-start | bytes 2359300
  20.1 4.1 %copy-start.2 = (f32[3,512]{1,0:T(4,128)S(1)}, f32[3,512]{1,0:T(4,128)}, u32[]{:S(2)}) copy-start(f32[3,512]{1,0:T(4,128)} %m_ref.1) | copy-start | bytes 18436
  20.1 4.1 %copy-start.3 = (f32[3,512]{1,0:T(4,128)S(1)}, f32[3,512]{1,0:T(4,128)}, u32[]{:S(2)}) copy-start(f32[3,512]{1,0:T(4,128)} %b_ref.1) | copy-start | bytes 18436

commit v3 on v2

--- a/solution.py
+++ b/solution.py
@@ -96,14 +96,27 @@
 
 
 def local_body(regions, domains, *refs):
-    sources, outputs, buffers, semaphores = refs[:5], refs[5:9], refs[9:14], refs[14]
+    sources, outputs, scratch, buffers, semaphores = refs[:7], refs[7:15], refs[15:19], refs[19:26], refs[26]
     fetch(sources, buffers, semaphores)
-    m_ref, dest_ref, nodes_ref, cell_ref, centers_ref = buffers
-    target_ref, hot_ref, cell_hot_ref, far_ref = outputs
+    m_ref, l_ref, b_ref, dest_ref, nodes_ref, cell_ref, centers_ref = buffers
+    target_ref, hot_ref, place_ref, own_ref, cell_hot_ref, far_ref, first_ref, second_ref = outputs
     count = m_ref.shape[1]
     cells = centers_ref.shape[1] // regions
     region = lax.axis_index("region")
     middle = middle_of(regions)
+    here = centers_ref[:, pl.ds(pl.multiple_of(region * cells, cells), cells)]
+    for k in range(1, regions):
+        other = lax.bitwise_xor(region, k)
+        there = centers_ref[:, pl.ds(pl.multiple_of(other * cells, cells), cells)]
+        column = jnp.transpose(jnp.concatenate([there, jnp.zeros((5, cells), F32)], axis=0))
+        d = [here[a : a + 1, :] - column[:, a : a + 1] for a in range(3)]
+        g1 = lax.rsqrt(d[0] * d[0] + d[1] * d[1] + d[2] * d[2] + CORE2)
+        g3 = g1 * g1 * g1
+        for j, factor in enumerate([g1] + [v * g3 for v in d]):
+            high, low = split2(factor)
+            row = ((k - 1) * 4 + j) * cells
+            far_ref[row : row + cells, 0:cells] = high.astype(BF16)
+            far_ref[row : row + cells, cells : 2 * cells] = low.astype(BF16)
     x = [m_ref[a : a + 1, :] - middle[a] for a in range(3)]
     parts = [split3(-2.0 * v) for v in x]
     norm = split3(x[0] * x[0] + x[1] * x[1] + x[2] * x[2] + CORE2)
@@ -120,32 +133,43 @@
     ).astype(BF16)
     before = dot(hot, earlier)
     rank = jnp.sum(before * hot.astype(F32), axis=0, keepdims=True).astype(jnp.int32)
-    slot = dest * LANES + rank
-    ids = jnp.concatenate([slot, nodes_ref[...], jnp.zeros((5, count), jnp.int32)], axis=0).astype(F32)
-    columns = jnp.transpose(ids).astype(jnp.int32)
-    slots = domains * LANES
-    wide = 1024
-    for start in range(0, hot_ref.shape[1], wide):
-        lane = lax.broadcasted_iota(jnp.int32, (count, wide), 1) + (start % slots if start < slots else start - slots)
-        if start < slots:
-            value = (lane == columns[:, 0:1]).astype(F32)
-        else:
-            value = 0.5 * (lane == columns[:, 1:2]).astype(F32) + 0.5 * (lane == columns[:, 2:3]).astype(F32)
-        hot_ref[:, start : start + wide] = value.astype(BF16)
+    nodes = nodes_ref[...]
+    place_ref[...] = jnp.concatenate([dest, nodes // LANES, jnp.zeros((5, count), jnp.int32)], axis=0)
+    columns = jnp.concatenate([rank, nodes % LANES, jnp.zeros((5, count), jnp.int32)], axis=0)
+    columns = jnp.transpose(columns.astype(F32)).astype(jnp.int32)
+    lane = lax.broadcasted_iota(jnp.int32, (count, LANES), 1)
+    for i in range(3):
+        hot_ref[:, i * LANES : (i + 1) * LANES] = (lane == columns[:, i : i + 1]).astype(BF16)
     cell_hot_ref[...] = (lax.broadcasted_iota(jnp.int32, (cells, count), 0) == cell_ref[...]).astype(BF16)
-    here = centers_ref[:, pl.ds(pl.multiple_of(region * cells, cells), cells)]
-    for k in range(1, regions):
-        other = lax.bitwise_xor(region, k)
-        there = centers_ref[:, pl.ds(pl.multiple_of(other * cells, cells), cells)]
-        column = jnp.transpose(jnp.concatenate([there, jnp.zeros((5, cells), F32)], axis=0))
-        d = [here[a : a + 1, :] - column[:, a : a + 1] for a in range(3)]
-        g1 = lax.rsqrt(d[0] * d[0] + d[1] * d[1] + d[2] * d[2] + CORE2)
-        g3 = g1 * g1 * g1
-        for j, factor in enumerate([g1] + [v * g3 for v in d]):
-            high, low = split2(factor)
-            row = ((k - 1) * 4 + j) * cells
-            far_ref[row : row + cells, 0:cells] = high.astype(BF16)
-            far_ref[row : row + cells, cells : 2 * cells] = low.astype(BF16)
+    own_ref[...] = jnp.concatenate(x + [b_ref[...], jnp.zeros((2, count), F32)], axis=0)
+    rows = source_terms(
+        x,
+        [l_ref[a : a + 1, :] for a in range(3)],
+        [b_ref[a : a + 1, :] for a in range(3)],
+        jnp.zeros((1, count), F32),
+    )
+    rows = jnp.concatenate(rows, axis=0)
+
+    def rows_of(step, start, size):
+        at = [(2 * step + h) * LANES for h in range(2)]
+        return [rows[start : start + size, i : i + LANES] for i in at]
+
+    first_ref[...] = jnp.zeros_like(first_ref)
+    second_ref[...] = jnp.zeros_like(second_ref)
+    pair_pipeline(rows_of, count // (2 * LANES), target_ref, first_ref, second_ref, scratch)
+
+
+def source_terms(m, l, b, cell):
+    q = [b[1] * l[2] - b[2] * l[1], b[2] * l[0] - b[0] * l[2], b[0] * l[1] - b[1] * l[0]]
+    outer = [b[i] * l[i] if i == j else 0.5 * (b[i] * l[j] + b[j] * l[i]) for i, j in SYM]
+    second = [q[i] * m[i] if i == j else 0.5 * (q[i] * m[j] + q[j] * m[i]) for i, j in SYM]
+    norm = m[0] * m[0] + m[1] * m[1] + m[2] * m[2]
+    zero, one = jnp.zeros_like(norm), jnp.ones_like(norm)
+    return m + [norm, one, cell, zero, zero] + outer + q + second + [zero]
+
+
+def block_of(device, quarter):
+    return (device // 8 * 4 + quarter) * 8 + device % 8
 
 
 def source_body(regions, got_ref, centers_ref, near_ref, moment_ref):
@@ -154,23 +178,19 @@
     devices = got_ref.shape[0] // sent_rows
     cells = moment_ref.shape[1]
     middle = middle_of(regions)
-    zero = jnp.zeros((8, LANES), F32)
-    one = jnp.ones((8, LANES), F32)
     for group in range(devices // 8):
         for quarter in range(quarters):
 
             def value(c):
                 return got_ref[pl.ds(group * 8 * sent_rows + c * quarters + quarter, 8, stride=sent_rows), :]
 
-            first_block = (group * quarters + quarter) * 8
-            m = [value(a) - middle[a] for a in range(3)]
-            l = [value(3 + a) for a in range(3)]
-            b = [value(6 + a) for a in range(3)]
-            q = [b[1] * l[2] - b[2] * l[1], b[2] * l[0] - b[0] * l[2], b[0] * l[1] - b[1] * l[0]]
-            outer = [b[i] * l[i] if i == j else 0.5 * (b[i] * l[j] + b[j] * l[i]) for i, j in SYM]
-            second = [q[i] * m[i] if i == j else 0.5 * (q[i] * m[j] + q[j] * m[i]) for i, j in SYM]
-            norm = m[0] * m[0] + m[1] * m[1] + m[2] * m[2]
-            rows = m + [norm, one, value(9), zero, zero] + outer + q + second + [zero]
+            first_block = block_of(group * 8, quarter)
+            rows = source_terms(
+                [value(a) - middle[a] for a in range(3)],
+                [value(3 + a) for a in range(3)],
+                [value(6 + a) for a in range(3)],
+                value(9),
+            )
             for f, row in enumerate(rows):
                 near_ref[pl.ds(first_block * SOURCE_ROWS + f, 8, stride=SOURCE_ROWS), :] = row
 
@@ -188,7 +208,7 @@
         return total + dot_nt(left, hot.astype(BF16))
 
     blocks = devices * quarters
-    total = lax.fori_loop(0, blocks // 2, step, jnp.zeros((120, cells), F32), unroll=4)
+    total = lax.fori_loop(0, blocks // 2, step, jnp.zeros((120, cells), F32), unroll=min(16, blocks // 2))
     total = total[0:40] + total[40:80] + total[80:120]
     region = lax.axis_index("region")
     here = centers_ref[:, pl.ds(pl.multiple_of(region * cells, cells), cells)]
@@ -208,15 +228,8 @@
         moment_ref[8 + 8 * a : 16 + 8 * a, :] = jnp.concatenate([about, pad], axis=0)
 
 
-def near_body(near_ref, target_ref, first_ref, second_ref, *scratch):
+def pair_pipeline(rows_of, length, target_ref, first_ref, second_ref, scratch):
     squares, factors = scratch[0:2], scratch[2:4]
-    steps = near_ref.shape[0] // SOURCE_ROWS // 2
-    first_ref[...] = jnp.zeros_like(first_ref)
-    second_ref[...] = jnp.zeros_like(second_ref)
-
-    def rows_of(step, start, size):
-        at = [(2 * step + h) * SOURCE_ROWS + start for h in range(2)]
-        return [near_ref[pl.ds(i if isinstance(i, int) else pl.multiple_of(i, 8), size), :] for i in at]
 
     def distances(step, slot):
         left = []
@@ -239,37 +252,57 @@
         left = jnp.concatenate([high, low], axis=0).astype(BF16)
         second_ref[...] += dot(left, factors[slot][2]) + dot(left, factors[slot][3])
 
-    def pipeline(first, length):
-        distances(first, 0)
-        distances(first + 1, 1)
-        powers(0)
-        for t in range(length):
-            if t + 2 < length:
-                distances(first + t + 2, t % 2)
-            if t + 1 < length:
-                powers((t + 1) % 2)
-            products(first + t, t % 2)
-
-    if steps <= PIPELINE:
-        pipeline(0, steps)
+    for t in range(min(2, length)):
+        distances(t, t)
+    powers(0)
+    for t in range(length):
+        if t + 2 < length:
+            distances(t + 2, t % 2)
+        if t + 1 < length:
+            powers((t + 1) % 2)
+        products(t, t % 2)
+
+
+def other_rows(near_ref, domains, first):
+    here = lax.axis_index("domain")
+
+    def rows_of(step, start, size):
+        step = first + step
+        device = lax.rem(here + 1 + step // 2, domains)
+        at = [block_of(device, step % 2 * 2 + h) * SOURCE_ROWS + start for h in range(2)]
+        return [near_ref[pl.ds(pl.multiple_of(i, 8), size), :] for i in at]
+
+    return rows_of
+
+
+def near_body(domains, steps, near_ref, target_ref, first_in, second_in, first_ref, second_ref, *scratch):
+    first_ref[...] = first_in[...]
+    second_ref[...] = second_in[...]
+    length = max(n for n in range(1, PIPELINE + 1) if steps % n == 0)
+
+    def run(first):
+        pair_pipeline(other_rows(near_ref, domains, first), length, target_ref, first_ref, second_ref, scratch)
+
+    if length == steps:
+        run(0)
     else:
 
         def part(i, carry):
-            pipeline(i * PIPELINE, PIPELINE)
+            run(i * length)
             return carry
 
-        lax.fori_loop(0, steps // PIPELINE, part, 0)
+        lax.fori_loop(0, steps // length, part, 0)
 
 
 def stacked3(x):
     return jnp.concatenate(split3(x), axis=0).astype(BF16)
 
 
-def force_body(regions, m_ref, b_ref, first_ref, second_ref, far_ref, cell_hot_ref, hot_ref, *rest):
-    moment_refs, out_ref = rest[:-1], rest[-1]
+def force_body(own, steps, last, near_ref, target_ref, first_in, second_in, own_ref, far_ref, cell_hot_ref, hot_ref, place_ref, *rest):
+    moment_refs, out_ref, scratch = rest[:-7], rest[-7], rest[-6:-2]
+    first_ref, second_ref = rest[-2:]
     cells = moment_refs[0].shape[1]
     domains = out_ref.shape[0]
-    middle = middle_of(regions)
     left = [ref[8 * j : 8 * j + 8, :] for ref in moment_refs for j in range(4)]
     left = stacked3(jnp.concatenate(left, axis=1))
     field = dot(left, far_ref[...])
@@ -277,40 +310,58 @@
     field = field[0:8] + field[8:16] + field[16:24]
     field = dot(stacked3(field), cell_hot_ref[...])
     field = field[0:8] + field[8:16] + field[16:24]
+    first_ref[...] = first_in[...]
+    second_ref[...] = second_in[...]
+    rows_of = other_rows(near_ref, domains, steps - last)
+    pair_pipeline(rows_of, last, target_ref, first_ref, second_ref, scratch)
     first = first_ref[...]
     second = second_ref[...]
     second = second[0:16] + second[16:32]
-    x = [m_ref[a : a + 1, :] - middle[a] for a in range(3)]
+    x = [own_ref[a : a + 1, :] for a in range(3)]
     q = [second[6 + a : 7 + a] for a in range(3)]
     cross = [q[i] * x[i] if i == j else 0.5 * (q[i] * x[j] + q[j] * x[i]) for i, j in SYM]
     sigma = first[0:6] + first[8:14] + (jnp.concatenate(cross, axis=0) - second[9:15]) + field[0:6]
     at = {}
     for row, (i, j) in enumerate(SYM):
         at[i, j] = at[j, i] = sigma[row : row + 1]
-    b = [b_ref[a : a + 1, :] for a in range(3)]
+    b = [own_ref[3 + a : 4 + a, :] for a in range(3)]
     force = [at[i, 0] * b[0] + at[i, 1] * b[1] + at[i, 2] * b[2] for i in range(3)]
-    force = jnp.concatenate(force + [jnp.zeros((5, b[0].shape[1]), F32)], axis=0)
-    spread = dot(stacked3(force), hot_ref[...])
-    spread = spread[0:3] + spread[8:11] + spread[16:19]
-    slots = domains * LANES
-    own = (spread.shape[1] - slots) // domains
+    none = jnp.zeros_like(b[0])
+
+    def spread(force, place, groups, i):
+        parts = [split2(v) for v in force]
+        rows = jnp.concatenate([v[0] for v in parts] + [none] + [v[1] for v in parts] + [none], axis=0)
+        left = [jnp.where(place == g, rows, 0.0) for g in range(groups)]
+        left = jnp.concatenate(left, axis=0).astype(BF16)
+        return dot(left, hot_ref[:, i * LANES : (i + 1) * LANES])
+
+    def joined(spread_rows, g):
+        return spread_rows[8 * g : 8 * g + 3] + spread_rows[8 * g + 4 : 8 * g + 7]
+
+    place = place_ref[...]
+    half = [0.5 * v for v in force]
+    halves = own // LANES
+    slots = spread(force, place[0:1], domains, 0)
+    ends = spread(half, place[1:2], domains * halves, 1) + spread(half, place[2:3], domains * halves, 2)
     for d in range(domains):
-        pieces = [spread[:, d * LANES : (d + 1) * LANES]]
-        for h in range(own // LANES):
-            pieces.append(spread[:, slots + d * own + h * LANES : slots + d * own + (h + 1) * LANES])
-        used = 3 * len(pieces)
-        pieces.append(jnp.zeros((out_ref.shape[1] - used, LANES), F32))
-        out_ref[d] = jnp.concatenate(pieces, axis=0)
+        pieces = [joined(slots, d)] + [joined(ends, d * halves + h) for h in range(halves)]
+        for i, piece in enumerate(pieces):
+            for a in range(3):
+                at = (3 * i + a) * LANES
+                out_ref[d, :, at : at + LANES] = piece[a : a + 1]
 
 
 def collect_body(got_ref, slot_ref, node_ref):
     domains = got_ref.shape[0]
     capacity = slot_ref.shape[1] // domains
-    total = jnp.sum(got_ref[...], axis=0)
-    for d in range(domains):
-        slot_ref[:, d * capacity : (d + 1) * capacity] = got_ref[d, 0:3, 0:capacity]
-    for h in range(node_ref.shape[1] // LANES):
-        node_ref[:, h * LANES : (h + 1) * LANES] = total[3 + 3 * h : 6 + 3 * h]
+    total = jnp.sum(got_ref[:, :, 3 * LANES :], axis=0)
+    for a in range(3):
+        for d in range(domains):
+            at = d * capacity
+            slot_ref[a : a + 1, at : at + capacity] = got_ref[d, :, a * LANES : a * LANES + capacity]
+        for h in range(node_ref.shape[1] // LANES):
+            at = (3 * h + a) * LANES
+            node_ref[a : a + 1, h * LANES : (h + 1) * LANES] = total[:, at : at + LANES]
 
 
 def body(midpoints, line_vectors, burgers, destination, node_ids, cell_ids, cell_centers):
@@ -318,8 +369,7 @@
     domains = lax.axis_size("domain")
     regions = lax.axis_size("region")
     cells = cell_centers.shape[1] // regions
-    nodes = count // 2 * domains
-    own = nodes // domains
+    own = count // 2
     cell_row = cell_ids.reshape(1, count)
     dest_row = destination.reshape(1, count)
     shape = jax.ShapeDtypeStruct
@@ -330,18 +380,24 @@
     )
     got = lax.all_to_all(payload, "domain", split_axis=0, concat_axis=0, tiled=True)
     far_rows = (regions - 1) * 4 * cells
-    inputs = (midpoints, dest_row, node_ids, cell_row, cell_centers)
-    target, hot, cell_hot, far = call(
+    pair_scratch = [pltpu.VMEM((2 * LANES, count), F32)] * 2 + [pltpu.VMEM((4, 2 * LANES, count), BF16)] * 2
+    sums = (pltpu.VMEM((FIRST_ROWS, count), F32), pltpu.VMEM((SECOND_ROWS, count), F32))
+    inputs = (midpoints, line_vectors, burgers, dest_row, node_ids, cell_row, cell_centers)
+    target, hot, place, own_rows, cell_hot, far, first, second = call(
         functools.partial(local_body, regions, domains),
         (
             pltpu.VMEM((DIST_ROWS, count), BF16),
-            pltpu.VMEM((count, domains * LANES + nodes), BF16),
+            pltpu.VMEM((count, 3 * LANES), BF16),
+            pltpu.VMEM((8, count), jnp.int32),
+            pltpu.VMEM((8, count), F32),
             pltpu.VMEM((cells, count), BF16),
             pltpu.VMEM((far_rows, 2 * cells), BF16),
-        ),
+        )
+        + sums,
         inputs,
         1 << 30,
         "local",
+        scratch=pair_scratch,
         fetched=inputs,
     )
     blocks = domains * quarters
@@ -355,21 +411,23 @@
     others = [
         lax.ppermute(moments, "region", [(r, r ^ k) for r in range(regions)]) for k in range(1, regions)
     ]
+    steps, last = (domains - 1) * quarters // 2, 2
     first, second = call(
-        near_body,
-        (pltpu.VMEM((FIRST_ROWS, count), F32), pltpu.VMEM((SECOND_ROWS, count), F32)),
-        (near, target),
+        functools.partial(near_body, domains, steps - last),
+        sums,
+        (near, target, first, second),
         1 << 32,
         "near",
-        scratch=[pltpu.VMEM((2 * LANES, count), F32)] * 2 + [pltpu.VMEM((4, 2 * LANES, count), BF16)] * 2,
-    )
-    rows = -(-(3 + 3 * (own // LANES)) // 8) * 8
+        scratch=pair_scratch,
+    )
+    sent = 3 * LANES + 3 * own
     outgoing = call(
-        functools.partial(force_body, regions),
-        shape((domains, rows, LANES), F32),
-        (midpoints, burgers, first, second, far, cell_hot, hot, *others),
+        functools.partial(force_body, own, steps, last),
+        shape((domains, 1, sent), F32),
+        (near, target, first, second, own_rows, far, cell_hot, hot, place, *others),
         1 << 28,
         "force",
+        scratch=pair_scratch + list(sums),
     )
     arrived = lax.all_to_all(outgoing, "domain", split_axis=0, concat_axis=0, tiled=True)
     return call(

time: 35.8 us -> 34.1 us (0.953)
  Pallas kernels: 11.2 us -> 9.05 us
  waiting for transfers between devices: 3.87 us -> 5.44 us
  local copies, waits for them, and re-layouts: 0.9 us -> 0.01 us
    pallas_call x6, Pallas kernels: 11.2 us -> 9.05 us  [call(): pl.pallas_call(body, out_shape=out_shape, in_specs=[space] * len(inputs),...]
    all_to_all x1, waiting for transfers between devices: 3.86 us -> 5.43 us  [body(): lax.all_to_all(payload, 'domain', split_axis=0, concat_axis=0, tiled=True)]
    unnamed x10 -> x2, local copies, waits for them, and re-layouts: 0.9 us -> 0.01 us
  transfers between devices with their start and end apart: 4 -> 4, of which waited for: 1 -> 1; matrix products, arithmetic and copies ran while one was open for 0% -> 0% of each run, Pallas kernels for 19% -> 15%
where the time goes in v3:
time: 34.1 us; the launch traced here: 33.8 us
  blocking collectives  9.34 us (27%)
  starting transfers between devices  9.24 us (27%)
  Pallas kernels  9.05 us (27%)
  waiting for transfers between devices  5.44 us (16%)
  between operations  0.7 us (2%)
    all_to_all x1, blocking collectives, body(): lax.all_to_all(outgoing, 'domain', split_axis=0, concat_axis=0, tiled=True)  9.34 us
    pallas_call x6, Pallas kernels, call(): pl.pallas_call(body, out_shape=out_shape, in_specs=[space] * len(inputs),...  9.05 us
    all_to_all x1, starting transfers between devices, body(): lax.all_to_all(payload, 'domain', split_axis=0, concat_axis=0, tiled=True)  7.32 us
    all_to_all x1, waiting for transfers between devices, body(): lax.all_to_all(payload, 'domain', split_axis=0, concat_axis=0, tiled=True)  5.43 us
    ppermute x3, starting transfers between devices, body(): lax.ppermute(moments, 'region', [(r, r ^ k) for r in range(regions)])  1.92 us
  transfers between devices with their start and end apart: 4, of which 1 were waited for; matrix products, arithmetic and copies ran while one was open for 0% of the time, Pallas kernels for 15%

profile of v3, /device:TPU:0, one launch (start us, length us, event | category | flops | bytes accessed | tf_op | source)
XLA Modules:
  0.0 33.8 jit_solution(4312310514492336801)
XLA Ops:
  0.6 1.4 %pack.1 = f32[8,40,128]{2,1,0:T(8,128)} custom-call(f32[3,512]{1,0:T(4,128)} %refs_0_.3, f32[3,512]{1,0:T(4,128)} %refs_1_.3, f32[3,512]{1,0:T(4,128)} %refs_2_.3, s32[1,512]{1,0:T(1,128)} %bitcast.4), custom_call_target="tpu_custom_call" | custom-call | flops 4096 | bytes 65536 | tf_op jit(solution)/shard_map/pack/pallas_call | solution.py:61
  2.1 7.3 %all-to-all-start = ((f32[8,40,128]{2,1,0:T(8,128)}), f32[8,40,128]{2,1,0:T(8,128)S(1)}, u32[]{:S(2)}, u32[]{:S(2)}) async-start(f32[8,40,128]{2,1,0:T(8,128)} %pack.1), calls=%async_computation | async-start | bytes 327680 | tf_op jit(solution)/shard_map/all_to_all | solution.py:381
  9.4 0.0 copy-start
  9.4 2.1 %local.1 = (bf16[48,512]{1,0:T(8,128)(2,1)S(1)}, bf16[512,384]{1,0:T(8,128)(2,1)S(1)}, s32[8,512]{1,0:T(8,128)S(1)}, f32[8,512]{1,0:T(8,128)S(1)}, bf16[128,512]...) custom-call(f32[3,512]{1,0:T(4,128)} %refs_0_.3, ...), custom_call_target="tpu_custom_call" | custom-call | flops 1073741824 | bytes 65536 | tf_op jit(solution)/shard_map/local/pallas_call | solution.py:61
  11.5 5.4 %all-to-all-done = f32[8,40,128]{2,1,0:T(8,128)S(1)} async-done(((f32[8,40,128]{2,1,0:T(8,128)}), f32[8,40,128]{2,1,0:T(8,128)S(1)}, u32[]{:S(2)}, u32[]{:S(2)}) %all-to-all-start) | async-done | bytes 163872 | tf_op jit(solution)/shard_map/all_to_all | solution.py:381
  17.0 0.0 copy-done
  17.0 0.6 %sources.1 = (f32[768,128]{1,0:T(8,128)S(1)}, f32[32,128]{1,0:T(8,128)S(1)}) custom-call(f32[320,128]{1,0:T(8,128)S(1)} %bitcast.3, f32[3,512]{1,0:T(4,128)S(1)} %copy-done), custom_call_target="tpu_custom_call" | custom-call | flops 268435456 | bytes 65536 | tf_op jit(solution)/shard_map/sources/pallas_call | solution.py:61
  17.5 0.1 collective-permute-start
  17.6 1.6 %collective-permute-start.1 = (f32[32,128]{1,0:T(8,128)S(1)}, f32[32,128]{1,0:T(8,128)S(1)}, u32[]{:S(2)}, u32[]{:S(2)}) collective-permute-start(f32[32,128]{1,0:T(8,128)S(1)} %get-tuple-element.25), channel_id=1, source_target_pairs={{0,16},{8,24},{16,0},{24,8},{1,17},{9,25},{17,1},{25,9},{2,18},{10... | collective-permute-start | bytes 49160 | tf_op jit(solution)/shard_map/ppermute | solution.py:412
  19.2 0.3 collective-permute-start.2
  19.5 3.1 %near.1 = (f32[16,512]{1,0:T(8,128)S(1)}, f32[32,512]{1,0:T(8,128)S(1)}) custom-call(f32[768,128]{1,0:T(8,128)S(1)} %get-tuple-element.14.near_ref, bf16[48,512]{1,0:T(8,128)(2,1)S(1)} %get-tuple-element.15.target_ref, f32[16,512]{1,0:T(8,128)S(1)} %get-tuple-element.16.first_in, f32[32,512]{1,0:T(8,128)S(1)} %get-tuple-element.17.second_in), custom_call_target="tpu_custom_call" | custom-call | flops 4294967296 | bytes 65536 | tf_op jit(solution)/shard_map/near/pallas_call | solution.py:61
  22.5 0.0 collective-permute-done.rest_0_
  22.5 0.0 collective-permute-done.1.rest_1_
  22.5 0.0 collective-permute-done.2.rest_2_
  22.5 1.2 %force.1 = f32[8,1,1152]{2,1,0:T(1,128)S(1)} custom-call(f32[768,128]{1,0:T(8,128)S(1)} %get-tuple-element.14.near_ref, bf16[48,512]{1,0:T(8,128)(2,1)S(1)} %get-tuple-element.15.target_ref, f32[16,512]{1,0:T(8,128)S(1)} %get-tuple-element.18.first_in, f32[32,512]{1,0:T(8,128)S(1)} %get-tuple-element.19.second_in, f32[8,512]{1,0:T(8,128)S(1)} %get-tuple-element.20.own_ref, ...), custom_call_target="tpu_custom_call" | custom-call | flops 268435456 | bytes 65536 | tf_op jit(solution)/shard_map/force/pallas_call | solution.py:61
  23.8 9.3 %all_to_all.10.got_ref = f32[8,1,1152]{2,1,0:T(1,128)S(1)} all-to-all(f32[8,1,1152]{2,1,0:T(1,128)S(1)} %force.1), channel_id=1, replica_groups=mesh['region'=4,'domain'=8] {'domain'}, dimensions={0} | all-to-all | bytes 73728 | tf_op jit(solution)/shard_map/all_to_all | solution.py:432
  33.1 0.6 %collect.1 = (f32[3,1024]{1,0:T(4,128)}, f32[3,256]{1,0:T(4,128)}) custom-call(f32[8,1,1152]{2,1,0:T(1,128)S(1)} %all_to_all.10.got_ref), custom_call_target="tpu_custom_call" | custom-call | flops 4096 | bytes 65536 | tf_op jit(solution)/shard_map/collect/pallas_call | solution.py:61
Async XLA Ops:
  2.1 14.9 %all-to-all-start = ((f32[8,40,128]{2,1,0:T(8,128)}), f32[8,40,128]{2,1,0:T(8,128)S(1)}, u32[]{:S(2)}, u32[]{:S(2)}) async-start(f32[8,40,128]{2,1,0:T(8,128)} %pack.1), calls=%async_computation | async-start | bytes 327680 | tf_op jit(solution)/shard_map/all_to_all | solution.py:381
  9.4 7.6 %copy-start = (f32[3,512]{1,0:T(4,128)S(1)}, f32[3,512]{1,0:T(4,128)}, u32[]{:S(2)}) copy-start(f32[3,512]{1,0:T(4,128)} %refs_6_.1) | copy-start | bytes 18436
  17.5 5.0 %collective-permute-start = (f32[32,128]{1,0:T(8,128)S(1)}, f32[32,128]{1,0:T(8,128)S(1)}, u32[]{:S(2)}, u32[]{:S(2)}) collective-permute-start(f32[32,128]{1,0:T(8,128)S(1)} %get-tuple-element.25), channel_id=1, source_target_pairs={{0,8},{8,0},{16,24},{24,16},{1,9},{9,1},{17,25},{25,17},{2,10},{10... | collective-permute-start | bytes 49160 | tf_op jit(solution)/shard_map/ppermute | solution.py:412
  17.6 4.9 %collective-permute-start.1 = (f32[32,128]{1,0:T(8,128)S(1)}, f32[32,128]{1,0:T(8,128)S(1)}, u32[]{:S(2)}, u32[]{:S(2)}) collective-permute-start(f32[32,128]{1,0:T(8,128)S(1)} %get-tuple-element.25), channel_id=1, source_target_pairs={{0,16},{8,24},{16,0},{24,8},{1,17},{9,25},{17,1},{25,9},{2,18},{10... | collective-permute-start | bytes 49160 | tf_op jit(solution)/shard_map/ppermute | solution.py:412
  19.2 3.4 %collective-permute-start.2 = (f32[32,128]{1,0:T(8,128)S(1)}, f32[32,128]{1,0:T(8,128)S(1)}, u32[]{:S(2)}, u32[]{:S(2)}) collective-permute-start(f32[32,128]{1,0:T(8,128)S(1)} %get-tuple-element.25), channel_id=1, source_target_pairs={{0,24},{8,16},{16,8},{24,0},{1,25},{9,17},{17,9},{25,1},{2,26},{10... | collective-permute-start | bytes 49160 | tf_op jit(solution)/shard_map/ppermute | solution.py:412

commit v4 on v3

--- a/solution.py
+++ b/solution.py
@@ -17,7 +17,7 @@
 DIST_ROWS = 48
 FIRST_ROWS, SECOND_ROWS = 16, 32
 PIPELINE = 16
-MOMENT_ROWS = 32
+MOMENT_ROWS = 24
 VMEM_LIMIT = 16 << 20
 VMEM_SPEC = pl.BlockSpec(memory_space=pltpu.VMEM)
 
@@ -220,45 +220,52 @@
         [none, n[1], none, 0.5 * n[0], none, 0.5 * n[2]],
         [none, none, n[2], none, 0.5 * n[0], 0.5 * n[1]],
     ]
-    pad = jnp.zeros((2, cells), F32)
-    moment_ref[0:8, :] = jnp.concatenate([charge, pad], axis=0)
+    groups = [charge]
     for a in range(3):
         about = total[8 + 8 * a : 14 + 8 * a] - (here[a : a + 1, :] - middle[a]) * charge
-        about = about + jnp.concatenate(fold[a], axis=0)
-        moment_ref[8 + 8 * a : 16 + 8 * a, :] = jnp.concatenate([about, pad], axis=0)
+        groups.append(about + jnp.concatenate(fold[a], axis=0))
+    moment_ref[...] = jnp.concatenate(groups, axis=0)
 
 
 def pair_pipeline(rows_of, length, target_ref, first_ref, second_ref, scratch):
     squares, factors = scratch[0:2], scratch[2:4]
 
-    def distances(step, slot):
+    wide = 256
+    halves = target_ref.shape[1] // wide
+
+    def distances(unit, slot):
+        step, at = unit // halves, unit % halves * wide
         left = []
         for part in rows_of(step, 0, 8):
             p = split3(part)
             left.append(jnp.transpose(jnp.concatenate([p[0], p[0], p[0], p[1], p[1], p[2]], axis=0)))
-        squares[slot][...] = dot(jnp.concatenate(left, axis=0).astype(BF16), target_ref[...])
+        left = jnp.concatenate(left, axis=0).astype(BF16)
+        squares[slot][:, 0:wide] = dot(left, target_ref[:, at : at + wide])
 
     def powers(slot):
-        g1 = lax.rsqrt(squares[slot][...])
+        g1 = lax.rsqrt(squares[slot][:, 0:wide])
         for k, g in ((0, g1), (2, g1 * g1 * g1)):
             high = g.astype(BF16)
-            factors[slot][k] = high
-            factors[slot][k + 1] = (g - high.astype(F32)).astype(BF16)
-
-    def products(step, slot):
+            factors[slot][k, :, 0:wide] = high
+            factors[slot][k + 1, :, 0:wide] = (g - high.astype(F32)).astype(BF16)
+
+    def products(unit, slot):
+        step, at = unit // halves, unit % halves * wide
+        f = [factors[slot][k, :, 0:wide] for k in range(4)]
         high, low = split2(jnp.concatenate(rows_of(step, 8, 16), axis=1))
         left = jnp.concatenate([high[0:8], low[0:8]], axis=0).astype(BF16)
-        first_ref[...] += dot(left, factors[slot][0]) + dot(left, factors[slot][1])
+        first_ref[:, at : at + wide] += dot(left, f[0]) + dot(left, f[1])
         left = jnp.concatenate([high, low], axis=0).astype(BF16)
-        second_ref[...] += dot(left, factors[slot][2]) + dot(left, factors[slot][3])
-
-    for t in range(min(2, length)):
+        second_ref[:, at : at + wide] += dot(left, f[2]) + dot(left, f[3])
+
+    units = length * halves
+    for t in range(min(2, units)):
         distances(t, t)
     powers(0)
-    for t in range(length):
-        if t + 2 < length:
+    for t in range(units):
+        if t + 2 < units:
             distances(t + 2, t % 2)
-        if t + 1 < length:
+        if t + 1 < units:
             powers((t + 1) % 2)
         products(t, t % 2)
 
@@ -303,8 +310,9 @@
     first_ref, second_ref = rest[-2:]
     cells = moment_refs[0].shape[1]
     domains = out_ref.shape[0]
-    left = [ref[8 * j : 8 * j + 8, :] for ref in moment_refs for j in range(4)]
-    left = stacked3(jnp.concatenate(left, axis=1))
+    left = [ref[6 * j : 6 * j + 6, :] for ref in moment_refs for j in range(4)]
+    left = jnp.concatenate(left, axis=1)
+    left = stacked3(jnp.concatenate([left, jnp.zeros((2, left.shape[1]), F32)], axis=0))
     field = dot(left, far_ref[...])
     field = field[:, 0:cells] + field[:, cells:]
     field = field[0:8] + field[8:16] + field[16:24]

time: 34.1 us -> 33.8 us (level)
  Pallas kernels: 9.05 us -> 8.7 us
    pallas_call x6, Pallas kernels: 9.05 us -> 8.7 us  [call(): pl.pallas_call(body, out_shape=out_shape, in_specs=[space] * len(inputs),...]
  transfers between devices with their start and end apart: 4 -> 4, of which waited for: 1 -> 2; matrix products, arithmetic and copies ran while one was open for 0% -> 0% of each run, Pallas kernels for 15% -> 14%
where the time goes in v4:
time: 33.8 us; the launch traced here: 33.5 us
  blocking collectives  9.35 us (28%)
  starting transfers between devices  9.24 us (27%)
  Pallas kernels  8.7 us (26%)
  waiting for transfers between devices  5.51 us (16%)
  between operations  0.69 us (2%)
    all_to_all x1, blocking collectives, body(): lax.all_to_all(outgoing, 'domain', split_axis=0, concat_axis=0, tiled=True)  9.35 us
    pallas_call x6, Pallas kernels, call(): pl.pallas_call(body, out_shape=out_shape, in_specs=[space] * len(inputs),...  8.7 us
    all_to_all x1, starting transfers between devices, body(): lax.all_to_all(payload, 'domain', split_axis=0, concat_axis=0, tiled=True)  7.32 us
    all_to_all x1, waiting for transfers between devices, body(): lax.all_to_all(payload, 'domain', split_axis=0, concat_axis=0, tiled=True)  5.4 us
    ppermute x3, starting transfers between devices, body(): lax.ppermute(moments, 'region', [(r, r ^ k) for r in range(regions)])  1.92 us
  transfers between devices with their start and end apart: 4, of which 2 were waited for; matrix products, arithmetic and copies ran while one was open for 0% of the time, Pallas kernels for 14%

profile of v4, /device:TPU:0, one launch (start us, length us, event | category | flops | bytes accessed | tf_op | source)
XLA Modules:
  0.0 33.5 jit_solution(3439148249183928381)
XLA Ops:
  0.6 1.4 %pack.1 = f32[8,40,128]{2,1,0:T(8,128)} custom-call(f32[3,512]{1,0:T(4,128)} %refs_0_.3, f32[3,512]{1,0:T(4,128)} %refs_1_.3, f32[3,512]{1,0:T(4,128)} %refs_2_.3, s32[1,512]{1,0:T(1,128)} %bitcast.4), custom_call_target="tpu_custom_call" | custom-call | flops 4096 | bytes 65536 | tf_op jit(solution)/shard_map/pack/pallas_call | solution.py:61
  2.1 7.3 %all-to-all-start = ((f32[8,40,128]{2,1,0:T(8,128)}), f32[8,40,128]{2,1,0:T(8,128)S(1)}, u32[]{:S(2)}, u32[]{:S(2)}) async-start(f32[8,40,128]{2,1,0:T(8,128)} %pack.1), calls=%async_computation | async-start | bytes 327680 | tf_op jit(solution)/shard_map/all_to_all | solution.py:389
  9.4 0.0 copy-start
  9.4 2.1 %local.1 = (bf16[48,512]{1,0:T(8,128)(2,1)S(1)}, bf16[512,384]{1,0:T(8,128)(2,1)S(1)}, s32[8,512]{1,0:T(8,128)S(1)}, f32[8,512]{1,0:T(8,128)S(1)}, bf16[128,512]...) custom-call(f32[3,512]{1,0:T(4,128)} %refs_0_.3, ...), custom_call_target="tpu_custom_call" | custom-call | flops 1073741824 | bytes 65536 | tf_op jit(solution)/shard_map/local/pallas_call | solution.py:61
  11.6 5.4 %all-to-all-done = f32[8,40,128]{2,1,0:T(8,128)S(1)} async-done(((f32[8,40,128]{2,1,0:T(8,128)}), f32[8,40,128]{2,1,0:T(8,128)S(1)}, u32[]{:S(2)}, u32[]{:S(2)}) %all-to-all-start) | async-done | bytes 163872 | tf_op jit(solution)/shard_map/all_to_all | solution.py:389
  17.0 0.0 copy-done
  17.0 0.6 %sources.1 = (f32[768,128]{1,0:T(8,128)S(1)}, f32[24,128]{1,0:T(8,128)S(1)}) custom-call(f32[320,128]{1,0:T(8,128)S(1)} %bitcast.3, f32[3,512]{1,0:T(4,128)S(1)} %copy-done), custom_call_target="tpu_custom_call" | custom-call | flops 268435456 | bytes 65536 | tf_op jit(solution)/shard_map/sources/pallas_call | solution.py:61
  17.5 0.1 collective-permute-start
  17.6 1.6 %collective-permute-start.1 = (f32[24,128]{1,0:T(8,128)S(1)}, f32[24,128]{1,0:T(8,128)S(1)}, u32[]{:S(2)}, u32[]{:S(2)}) collective-permute-start(f32[24,128]{1,0:T(8,128)S(1)} %get-tuple-element.25), channel_id=1, source_target_pairs={{0,16},{8,24},{16,0},{24,8},{1,17},{9,25},{17,1},{25,9},{2,18},{10... | collective-permute-start | bytes 36872 | tf_op jit(solution)/shard_map/ppermute | solution.py:420
  19.2 0.3 collective-permute-start.2
  19.5 2.7 %near.1 = (f32[16,512]{1,0:T(8,128)S(1)}, f32[32,512]{1,0:T(8,128)S(1)}) custom-call(f32[768,128]{1,0:T(8,128)S(1)} %get-tuple-element.14.near_ref, bf16[48,512]{1,0:T(8,128)(2,1)S(1)} %get-tuple-element.15.target_ref, f32[16,512]{1,0:T(8,128)S(1)} %get-tuple-element.16.first_in, f32[32,512]{1,0:T(8,128)S(1)} %get-tuple-element.17.second_in), custom_call_target="tpu_custom_call" | custom-call | flops 4294967296 | bytes 65536 | tf_op jit(solution)/shard_map/near/pallas_call | solution.py:61
  22.2 0.0 collective-permute-done.rest_0_
  22.2 0.0 collective-permute-done.1.rest_1_
  22.2 0.1 collective-permute-done.2.rest_2_
  22.3 1.2 %force.1 = f32[8,1,1152]{2,1,0:T(1,128)S(1)} custom-call(f32[768,128]{1,0:T(8,128)S(1)} %get-tuple-element.14.near_ref, bf16[48,512]{1,0:T(8,128)(2,1)S(1)} %get-tuple-element.15.target_ref, f32[16,512]{1,0:T(8,128)S(1)} %get-tuple-element.18.first_in, f32[32,512]{1,0:T(8,128)S(1)} %get-tuple-element.19.second_in, f32[8,512]{1,0:T(8,128)S(1)} %get-tuple-element.20.own_ref, ...), custom_call_target="tpu_custom_call" | custom-call | flops 268435456 | bytes 65536 | tf_op jit(solution)/shard_map/force/pallas_call | solution.py:61
  23.5 9.3 %all_to_all.10.got_ref = f32[8,1,1152]{2,1,0:T(1,128)S(1)} all-to-all(f32[8,1,1152]{2,1,0:T(1,128)S(1)} %force.1), channel_id=1, replica_groups=mesh['region'=4,'domain'=8] {'domain'}, dimensions={0} | all-to-all | bytes 73728 | tf_op jit(solution)/shard_map/all_to_all | solution.py:440
  32.9 0.6 %collect.1 = (f32[3,1024]{1,0:T(4,128)}, f32[3,256]{1,0:T(4,128)}) custom-call(f32[8,1,1152]{2,1,0:T(1,128)S(1)} %all_to_all.10.got_ref), custom_call_target="tpu_custom_call" | custom-call | flops 4096 | bytes 65536 | tf_op jit(solution)/shard_map/collect/pallas_call | solution.py:61
Async XLA Ops:
  2.1 14.9 %all-to-all-start = ((f32[8,40,128]{2,1,0:T(8,128)}), f32[8,40,128]{2,1,0:T(8,128)S(1)}, u32[]{:S(2)}, u32[]{:S(2)}) async-start(f32[8,40,128]{2,1,0:T(8,128)} %pack.1), calls=%async_computation | async-start | bytes 327680 | tf_op jit(solution)/shard_map/all_to_all | solution.py:389
  9.4 7.6 %copy-start = (f32[3,512]{1,0:T(4,128)S(1)}, f32[3,512]{1,0:T(4,128)}, u32[]{:S(2)}) copy-start(f32[3,512]{1,0:T(4,128)} %refs_6_.1) | copy-start | bytes 18436
  17.5 4.6 %collective-permute-start = (f32[24,128]{1,0:T(8,128)S(1)}, f32[24,128]{1,0:T(8,128)S(1)}, u32[]{:S(2)}, u32[]{:S(2)}) collective-permute-start(f32[24,128]{1,0:T(8,128)S(1)} %get-tuple-element.25), channel_id=1, source_target_pairs={{0,8},{8,0},{16,24},{24,16},{1,9},{9,1},{17,25},{25,17},{2,10},{10... | collective-permute-start | bytes 36872 | tf_op jit(solution)/shard_map/ppermute | solution.py:420
  17.6 4.6 %collective-permute-start.1 = (f32[24,128]{1,0:T(8,128)S(1)}, f32[24,128]{1,0:T(8,128)S(1)}, u32[]{:S(2)}, u32[]{:S(2)}) collective-permute-start(f32[24,128]{1,0:T(8,128)S(1)} %get-tuple-element.25), channel_id=1, source_target_pairs={{0,16},{8,24},{16,0},{24,8},{1,17},{9,25},{17,1},{25,9},{2,18},{10... | collective-permute-start | bytes 36872 | tf_op jit(solution)/shard_map/ppermute | solution.py:420
  19.2 3.1 %collective-permute-start.2 = (f32[24,128]{1,0:T(8,128)S(1)}, f32[24,128]{1,0:T(8,128)S(1)}, u32[]{:S(2)}, u32[]{:S(2)}) collective-permute-start(f32[24,128]{1,0:T(8,128)S(1)} %get-tuple-element.25), channel_id=1, source_target_pairs={{0,24},{8,16},{16,8},{24,0},{1,25},{9,17},{17,9},{25,1},{2,26},{10... | collective-permute-start | bytes 36872 | tf_op jit(solution)/shard_map/ppermute | solution.py:420

commit v5 on v4

--- a/solution.py
+++ b/solution.py
@@ -305,12 +305,12 @@
     return jnp.concatenate(split3(x), axis=0).astype(BF16)
 
 
-def force_body(own, steps, last, near_ref, target_ref, first_in, second_in, own_ref, far_ref, cell_hot_ref, hot_ref, place_ref, *rest):
+def force_body(own, order, steps, last, near_ref, target_ref, first_in, second_in, own_ref, far_ref, cell_hot_ref, hot_ref, place_ref, *rest):
     moment_refs, out_ref, scratch = rest[:-7], rest[-7], rest[-6:-2]
     first_ref, second_ref = rest[-2:]
     cells = moment_refs[0].shape[1]
     domains = out_ref.shape[0]
-    left = [ref[6 * j : 6 * j + 6, :] for ref in moment_refs for j in range(4)]
+    left = [ref[6 * j : 6 * j + 6, :] for k in sorted(order) for ref in [moment_refs[order.index(k)]] for j in range(4)]
     left = jnp.concatenate(left, axis=1)
     left = stacked3(jnp.concatenate([left, jnp.zeros((2, left.shape[1]), F32)], axis=0))
     field = dot(left, far_ref[...])
@@ -416,9 +416,8 @@
         1 << 28,
         "sources",
     )
-    others = [
-        lax.ppermute(moments, "region", [(r, r ^ k) for r in range(regions)]) for k in range(1, regions)
-    ]
+    order = sorted(range(1, regions), key=lambda k: -k)
+    others = [lax.ppermute(moments, "region", [(r, r ^ k) for r in range(regions)]) for k in order]
     steps, last = (domains - 1) * quarters // 2, 2
     first, second = call(
         functools.partial(near_body, domains, steps - last),
@@ -430,7 +429,7 @@
     )
     sent = 3 * LANES + 3 * own
     outgoing = call(
-        functools.partial(force_body, own, steps, last),
+        functools.partial(force_body, own, order, steps, last),
         shape((domains, 1, sent), F32),
         (near, target, first, second, own_rows, far, cell_hot, hot, place, *others),
         1 << 28,

time: 33.8 us -> 33.8 us (level)
  transfers between devices with their start and end apart: 4 -> 4, of which waited for: 2 -> 1; matrix products, arithmetic and copies ran while one was open for 0% -> 0% of each run, Pallas kernels for 14% -> 15%
where the time goes in v5:
time: 33.8 us; the launch traced here: 33.4 us
  blocking collectives  9.35 us (28%)
  starting transfers between devices  9.24 us (27%)
  Pallas kernels  8.7 us (26%)
  waiting for transfers between devices  5.41 us (16%)
  between operations  0.7 us (2%)
    all_to_all x1, blocking collectives, body(): lax.all_to_all(outgoing, 'domain', split_axis=0, concat_axis=0, tiled=True)  9.35 us
    pallas_call x6, Pallas kernels, call(): pl.pallas_call(body, out_shape=out_shape, in_specs=[space] * len(inputs),...  8.7 us
    all_to_all x1, starting transfers between devices, body(): lax.all_to_all(payload, 'domain', split_axis=0, concat_axis=0, tiled=True)  7.32 us
    all_to_all x1, waiting for transfers between devices, body(): lax.all_to_all(payload, 'domain', split_axis=0, concat_axis=0, tiled=True)  5.4 us
    ppermute x3, starting transfers between devices, body(): lax.ppermute(moments, 'region', [(r, r ^ k) for r in range(regions)])  1.92 us
  transfers between devices with their start and end apart: 4, of which 1 were waited for; matrix products, arithmetic and copies ran while one was open for 0% of the time, Pallas kernels for 15%

profile of v5, /device:TPU:0, one launch (start us, length us, event | category | flops | bytes accessed | tf_op | source)
XLA Modules:
  0.0 33.4 jit_solution(6656926153511592594)
XLA Ops:
  0.6 1.4 %pack.1 = f32[8,40,128]{2,1,0:T(8,128)} custom-call(f32[3,512]{1,0:T(4,128)} %refs_0_.3, f32[3,512]{1,0:T(4,128)} %refs_1_.3, f32[3,512]{1,0:T(4,128)} %refs_2_.3, s32[1,512]{1,0:T(1,128)} %bitcast.4), custom_call_target="tpu_custom_call" | custom-call | flops 4096 | bytes 65536 | tf_op jit(solution)/shard_map/pack/pallas_call | solution.py:61
  2.1 7.3 %all-to-all-start = ((f32[8,40,128]{2,1,0:T(8,128)}), f32[8,40,128]{2,1,0:T(8,128)S(1)}, u32[]{:S(2)}, u32[]{:S(2)}) async-start(f32[8,40,128]{2,1,0:T(8,128)} %pack.1), calls=%async_computation | async-start | bytes 327680 | tf_op jit(solution)/shard_map/all_to_all | solution.py:389
  9.4 0.0 copy-start
  9.4 2.1 %local.1 = (bf16[48,512]{1,0:T(8,128)(2,1)S(1)}, bf16[512,384]{1,0:T(8,128)(2,1)S(1)}, s32[8,512]{1,0:T(8,128)S(1)}, f32[8,512]{1,0:T(8,128)S(1)}, bf16[128,512]...) custom-call(f32[3,512]{1,0:T(4,128)} %refs_0_.3, ...), custom_call_target="tpu_custom_call" | custom-call | flops 1073741824 | bytes 65536 | tf_op jit(solution)/shard_map/local/pallas_call | solution.py:61
  11.6 5.4 %all-to-all-done = f32[8,40,128]{2,1,0:T(8,128)S(1)} async-done(((f32[8,40,128]{2,1,0:T(8,128)}), f32[8,40,128]{2,1,0:T(8,128)S(1)}, u32[]{:S(2)}, u32[]{:S(2)}) %all-to-all-start) | async-done | bytes 163872 | tf_op jit(solution)/shard_map/all_to_all | solution.py:389
  17.0 0.0 copy-done
  17.0 0.6 %sources.1 = (f32[768,128]{1,0:T(8,128)S(1)}, f32[24,128]{1,0:T(8,128)S(1)}) custom-call(f32[320,128]{1,0:T(8,128)S(1)} %bitcast.3, f32[3,512]{1,0:T(4,128)S(1)} %copy-done), custom_call_target="tpu_custom_call" | custom-call | flops 268435456 | bytes 65536 | tf_op jit(solution)/shard_map/sources/pallas_call | solution.py:61
  17.5 0.1 collective-permute-start
  17.6 1.6 %collective-permute-start.1 = (f32[24,128]{1,0:T(8,128)S(1)}, f32[24,128]{1,0:T(8,128)S(1)}, u32[]{:S(2)}, u32[]{:S(2)}) collective-permute-start(f32[24,128]{1,0:T(8,128)S(1)} %get-tuple-element.25), channel_id=1, source_target_pairs={{0,16},{8,24},{16,0},{24,8},{1,17},{9,25},{17,1},{25,9},{2,18},{10... | collective-permute-start | bytes 36872 | tf_op jit(solution)/shard_map/ppermute | solution.py:420
  19.2 0.3 collective-permute-start.2
  19.5 2.7 %near.1 = (f32[16,512]{1,0:T(8,128)S(1)}, f32[32,512]{1,0:T(8,128)S(1)}) custom-call(f32[768,128]{1,0:T(8,128)S(1)} %get-tuple-element.14.near_ref, bf16[48,512]{1,0:T(8,128)(2,1)S(1)} %get-tuple-element.15.target_ref, f32[16,512]{1,0:T(8,128)S(1)} %get-tuple-element.16.first_in, f32[32,512]{1,0:T(8,128)S(1)} %get-tuple-element.17.second_in), custom_call_target="tpu_custom_call" | custom-call | flops 4294967296 | bytes 65536 | tf_op jit(solution)/shard_map/near/pallas_call | solution.py:61
  22.2 0.0 collective-permute-done.rest_0_
  22.2 0.0 collective-permute-done.1.rest_1_
  22.2 0.0 collective-permute-done.2.rest_2_
  22.2 1.2 %force.1 = f32[8,1,1152]{2,1,0:T(1,128)S(1)} custom-call(f32[768,128]{1,0:T(8,128)S(1)} %get-tuple-element.14.near_ref, bf16[48,512]{1,0:T(8,128)(2,1)S(1)} %get-tuple-element.15.target_ref, f32[16,512]{1,0:T(8,128)S(1)} %get-tuple-element.18.first_in, f32[32,512]{1,0:T(8,128)S(1)} %get-tuple-element.19.second_in, f32[8,512]{1,0:T(8,128)S(1)} %get-tuple-element.20.own_ref, ...), custom_call_target="tpu_custom_call" | custom-call | flops 268435456 | bytes 65536 | tf_op jit(solution)/shard_map/force/pallas_call | solution.py:61
  23.4 9.3 %all_to_all.10.got_ref = f32[8,1,1152]{2,1,0:T(1,128)S(1)} all-to-all(f32[8,1,1152]{2,1,0:T(1,128)S(1)} %force.1), channel_id=1, replica_groups=mesh['region'=4,'domain'=8] {'domain'}, dimensions={0} | all-to-all | bytes 73728 | tf_op jit(solution)/shard_map/all_to_all | solution.py:439
  32.8 0.6 %collect.1 = (f32[3,1024]{1,0:T(4,128)}, f32[3,256]{1,0:T(4,128)}) custom-call(f32[8,1,1152]{2,1,0:T(1,128)S(1)} %all_to_all.10.got_ref), custom_call_target="tpu_custom_call" | custom-call | flops 4096 | bytes 65536 | tf_op jit(solution)/shard_map/collect/pallas_call | solution.py:61
Async XLA Ops:
  2.1 14.9 %all-to-all-start = ((f32[8,40,128]{2,1,0:T(8,128)}), f32[8,40,128]{2,1,0:T(8,128)S(1)}, u32[]{:S(2)}, u32[]{:S(2)}) async-start(f32[8,40,128]{2,1,0:T(8,128)} %pack.1), calls=%async_computation | async-start | bytes 327680 | tf_op jit(solution)/shard_map/all_to_all | solution.py:389
  9.4 7.6 %copy-start = (f32[3,512]{1,0:T(4,128)S(1)}, f32[3,512]{1,0:T(4,128)}, u32[]{:S(2)}) copy-start(f32[3,512]{1,0:T(4,128)} %refs_6_.1) | copy-start | bytes 18436
  17.5 4.6 %collective-permute-start = (f32[24,128]{1,0:T(8,128)S(1)}, f32[24,128]{1,0:T(8,128)S(1)}, u32[]{:S(2)}, u32[]{:S(2)}) collective-permute-start(f32[24,128]{1,0:T(8,128)S(1)} %get-tuple-element.25), channel_id=1, source_target_pairs={{0,24},{8,16},{16,8},{24,0},{1,25},{9,17},{17,9},{25,1},{2,26},{10... | collective-permute-start | bytes 36872 | tf_op jit(solution)/shard_map/ppermute | solution.py:420
  17.6 4.6 %collective-permute-start.1 = (f32[24,128]{1,0:T(8,128)S(1)}, f32[24,128]{1,0:T(8,128)S(1)}, u32[]{:S(2)}, u32[]{:S(2)}) collective-permute-start(f32[24,128]{1,0:T(8,128)S(1)} %get-tuple-element.25), channel_id=1, source_target_pairs={{0,16},{8,24},{16,0},{24,8},{1,17},{9,25},{17,1},{25,9},{2,18},{10... | collective-permute-start | bytes 36872 | tf_op jit(solution)/shard_map/ppermute | solution.py:420
  19.2 3.0 %collective-permute-start.2 = (f32[24,128]{1,0:T(8,128)S(1)}, f32[24,128]{1,0:T(8,128)S(1)}, u32[]{:S(2)}, u32[]{:S(2)}) collective-permute-start(f32[24,128]{1,0:T(8,128)S(1)} %get-tuple-element.25), channel_id=1, source_target_pairs={{0,8},{8,0},{16,24},{24,16},{1,9},{9,1},{17,25},{25,17},{2,10},{10... | collective-permute-start | bytes 36872 | tf_op jit(solution)/shard_map/ppermute | solution.py:420

commit v6 on v5

--- a/solution.py
+++ b/solution.py
@@ -418,7 +418,7 @@
     )
     order = sorted(range(1, regions), key=lambda k: -k)
     others = [lax.ppermute(moments, "region", [(r, r ^ k) for r in range(regions)]) for k in order]
-    steps, last = (domains - 1) * quarters // 2, 2
+    steps, last = (domains - 1) * quarters // 2, 4
     first, second = call(
         functools.partial(near_body, domains, steps - last),
         sums,

time: 33.8 us -> 34 us (level)
  transfers between devices with their start and end apart: 4 -> 4, of which waited for: 1 -> 1; matrix products, arithmetic and copies ran while one was open for 0% -> 0% of each run, Pallas kernels for 15% -> 13%
where the time goes in v6:
time: 34 us; the launch traced here: 33.6 us
  blocking collectives  9.58 us (28%)
  starting transfers between devices  9.24 us (27%)
  Pallas kernels  8.71 us (26%)
  waiting for transfers between devices  5.41 us (16%)
  between operations  0.7 us (2%)
    all_to_all x1, blocking collectives, body(): lax.all_to_all(outgoing, 'domain', split_axis=0, concat_axis=0, tiled=True)  9.58 us
    pallas_call x6, Pallas kernels, call(): pl.pallas_call(body, out_shape=out_shape, in_specs=[space] * len(inputs),...  8.71 us
    all_to_all x1, starting transfers between devices, body(): lax.all_to_all(payload, 'domain', split_axis=0, concat_axis=0, tiled=True)  7.32 us
    all_to_all x1, waiting for transfers between devices, body(): lax.all_to_all(payload, 'domain', split_axis=0, concat_axis=0, tiled=True)  5.4 us
    ppermute x3, starting transfers between devices, body(): lax.ppermute(moments, 'region', [(r, r ^ k) for r in range(regions)])  1.92 us
  transfers between devices with their start and end apart: 4, of which 1 were waited for; matrix products, arithmetic and copies ran while one was open for 0% of the time, Pallas kernels for 13%

profile of v6, /device:TPU:0, one launch (start us, length us, event | category | flops | bytes accessed | tf_op | source)
XLA Modules:
  0.0 33.6 jit_solution(9468485145071152268)
XLA Ops:
  0.6 1.4 %pack.1 = f32[8,40,128]{2,1,0:T(8,128)} custom-call(f32[3,512]{1,0:T(4,128)} %refs_0_.3, f32[3,512]{1,0:T(4,128)} %refs_1_.3, f32[3,512]{1,0:T(4,128)} %refs_2_.3, s32[1,512]{1,0:T(1,128)} %bitcast.4), custom_call_target="tpu_custom_call" | custom-call | flops 4096 | bytes 65536 | tf_op jit(solution)/shard_map/pack/pallas_call | solution.py:61
  2.1 7.3 %all-to-all-start = ((f32[8,40,128]{2,1,0:T(8,128)}), f32[8,40,128]{2,1,0:T(8,128)S(1)}, u32[]{:S(2)}, u32[]{:S(2)}) async-start(f32[8,40,128]{2,1,0:T(8,128)} %pack.1), calls=%async_computation | async-start | bytes 327680 | tf_op jit(solution)/shard_map/all_to_all | solution.py:389
  9.4 0.0 copy-start
  9.4 2.1 %local.1 = (bf16[48,512]{1,0:T(8,128)(2,1)S(1)}, bf16[512,384]{1,0:T(8,128)(2,1)S(1)}, s32[8,512]{1,0:T(8,128)S(1)}, f32[8,512]{1,0:T(8,128)S(1)}, bf16[128,512]...) custom-call(f32[3,512]{1,0:T(4,128)} %refs_0_.3, ...), custom_call_target="tpu_custom_call" | custom-call | flops 1073741824 | bytes 65536 | tf_op jit(solution)/shard_map/local/pallas_call | solution.py:61
  11.6 5.4 %all-to-all-done = f32[8,40,128]{2,1,0:T(8,128)S(1)} async-done(((f32[8,40,128]{2,1,0:T(8,128)}), f32[8,40,128]{2,1,0:T(8,128)S(1)}, u32[]{:S(2)}, u32[]{:S(2)}) %all-to-all-start) | async-done | bytes 163872 | tf_op jit(solution)/shard_map/all_to_all | solution.py:389
  17.0 0.0 copy-done
  17.0 0.6 %sources.1 = (f32[768,128]{1,0:T(8,128)S(1)}, f32[24,128]{1,0:T(8,128)S(1)}) custom-call(f32[320,128]{1,0:T(8,128)S(1)} %bitcast.3, f32[3,512]{1,0:T(4,128)S(1)} %copy-done), custom_call_target="tpu_custom_call" | custom-call | flops 268435456 | bytes 65536 | tf_op jit(solution)/shard_map/sources/pallas_call | solution.py:61
  17.5 0.1 collective-permute-start
  17.6 1.6 %collective-permute-start.1 = (f32[24,128]{1,0:T(8,128)S(1)}, f32[24,128]{1,0:T(8,128)S(1)}, u32[]{:S(2)}, u32[]{:S(2)}) collective-permute-start(f32[24,128]{1,0:T(8,128)S(1)} %get-tuple-element.25), channel_id=1, source_target_pairs={{0,16},{8,24},{16,0},{24,8},{1,17},{9,25},{17,1},{25,9},{2,18},{10... | collective-permute-start | bytes 36872 | tf_op jit(solution)/shard_map/ppermute | solution.py:420
  19.2 0.3 collective-permute-start.2
  19.5 2.3 %near.1 = (f32[16,512]{1,0:T(8,128)S(1)}, f32[32,512]{1,0:T(8,128)S(1)}) custom-call(f32[768,128]{1,0:T(8,128)S(1)} %get-tuple-element.14.near_ref, bf16[48,512]{1,0:T(8,128)(2,1)S(1)} %get-tuple-element.15.target_ref, f32[16,512]{1,0:T(8,128)S(1)} %get-tuple-element.16.first_in, f32[32,512]{1,0:T(8,128)S(1)} %get-tuple-element.17.second_in), custom_call_target="tpu_custom_call" | custom-call | flops 4294967296 | bytes 65536 | tf_op jit(solution)/shard_map/near/pallas_call | solution.py:61
  21.8 0.0 collective-permute-done.rest_0_
  21.8 0.0 collective-permute-done.1.rest_1_
  21.8 0.0 collective-permute-done.2.rest_2_
  21.8 1.6 %force.1 = f32[8,1,1152]{2,1,0:T(1,128)S(1)} custom-call(f32[768,128]{1,0:T(8,128)S(1)} %get-tuple-element.14.near_ref, bf16[48,512]{1,0:T(8,128)(2,1)S(1)} %get-tuple-element.15.target_ref, f32[16,512]{1,0:T(8,128)S(1)} %get-tuple-element.18.first_in, f32[32,512]{1,0:T(8,128)S(1)} %get-tuple-element.19.second_in, f32[8,512]{1,0:T(8,128)S(1)} %get-tuple-element.20.own_ref, ...), custom_call_target="tpu_custom_call" | custom-call | flops 268435456 | bytes 65536 | tf_op jit(solution)/shard_map/force/pallas_call | solution.py:61
  23.4 9.6 %all_to_all.10.got_ref = f32[8,1,1152]{2,1,0:T(1,128)S(1)} all-to-all(f32[8,1,1152]{2,1,0:T(1,128)S(1)} %force.1), channel_id=1, replica_groups=mesh['region'=4,'domain'=8] {'domain'}, dimensions={0} | all-to-all | bytes 73728 | tf_op jit(solution)/shard_map/all_to_all | solution.py:439
  33.0 0.6 %collect.1 = (f32[3,1024]{1,0:T(4,128)}, f32[3,256]{1,0:T(4,128)}) custom-call(f32[8,1,1152]{2,1,0:T(1,128)S(1)} %all_to_all.10.got_ref), custom_call_target="tpu_custom_call" | custom-call | flops 4096 | bytes 65536 | tf_op jit(solution)/shard_map/collect/pallas_call | solution.py:61
Async XLA Ops:
  2.1 14.9 %all-to-all-start = ((f32[8,40,128]{2,1,0:T(8,128)}), f32[8,40,128]{2,1,0:T(8,128)S(1)}, u32[]{:S(2)}, u32[]{:S(2)}) async-start(f32[8,40,128]{2,1,0:T(8,128)} %pack.1), calls=%async_computation | async-start | bytes 327680 | tf_op jit(solution)/shard_map/all_to_all | solution.py:389
  9.4 7.6 %copy-start = (f32[3,512]{1,0:T(4,128)S(1)}, f32[3,512]{1,0:T(4,128)}, u32[]{:S(2)}) copy-start(f32[3,512]{1,0:T(4,128)} %refs_6_.1) | copy-start | bytes 18436
  17.5 4.3 %collective-permute-start = (f32[24,128]{1,0:T(8,128)S(1)}, f32[24,128]{1,0:T(8,128)S(1)}, u32[]{:S(2)}, u32[]{:S(2)}) collective-permute-start(f32[24,128]{1,0:T(8,128)S(1)} %get-tuple-element.25), channel_id=1, source_target_pairs={{0,24},{8,16},{16,8},{24,0},{1,25},{9,17},{17,9},{25,1},{2,26},{10... | collective-permute-start | bytes 36872 | tf_op jit(solution)/shard_map/ppermute | solution.py:420
  17.6 4.2 %collective-permute-start.1 = (f32[24,128]{1,0:T(8,128)S(1)}, f32[24,128]{1,0:T(8,128)S(1)}, u32[]{:S(2)}, u32[]{:S(2)}) collective-permute-start(f32[24,128]{1,0:T(8,128)S(1)} %get-tuple-element.25), channel_id=1, source_target_pairs={{0,16},{8,24},{16,0},{24,8},{1,17},{9,25},{17,1},{25,9},{2,18},{10... | collective-permute-start | bytes 36872 | tf_op jit(solution)/shard_map/ppermute | solution.py:420
  19.2 2.7 %collective-permute-start.2 = (f32[24,128]{1,0:T(8,128)S(1)}, f32[24,128]{1,0:T(8,128)S(1)}, u32[]{:S(2)}, u32[]{:S(2)}) collective-permute-start(f32[24,128]{1,0:T(8,128)S(1)} %get-tuple-element.25), channel_id=1, source_target_pairs={{0,8},{8,0},{16,24},{24,16},{1,9},{9,1},{17,25},{25,17},{2,10},{10... | collective-permute-start | bytes 36872 | tf_op jit(solution)/shard_map/ppermute | solution.py:420
